TPU v7x, 512 devices: a whole 4x4x16 slice. The times are simulated.
512 devices in a mesh: wide: 128 (over x, z, core), narrow: 4 (over y).
Axes of the slice: x: 4, y: 4, z: 16, core: 2. Of those that a mesh axis runs over, the one named last changes fastest.
Arguments:
- queries: bfloat16 [65536, 2048], P(('wide', 'narrow')), may hold values from -12 to 12
- keys: bfloat16 [65536, 2048], P(('wide', 'narrow')), may hold values from -24 to 24
- values: bfloat16 [65536, 2048], P(('wide', 'narrow')), may hold values from -6 to 6
- view_lengths: int32 [128, 4], P('wide'), may hold values from 1 to 256, 512 in all within a row
- gain: float32 [2048], replicated, may hold values from 0.25 to 1.75
- w_gate: bfloat16 [4, 512, 512], P('narrow', 'wide'), may hold values from -0.25 to 0.25
- w_up: bfloat16 [4, 512, 512], P('narrow', 'wide'), may hold values from -0.25 to 0.25
- w_down: bfloat16 [4, 512, 512], P('narrow', 'wide'), may hold values from -0.25 to 0.25
- m_gate: float32 [4, 512, 512], P('narrow', 'wide'), may hold values from -4 to 4
- m_up: float32 [4, 512, 512], P('narrow', 'wide'), may hold values from -4 to 4
- m_down: float32 [4, 512, 512], P('narrow', 'wide'), may hold values from -4 to 4
Outputs:
- output: bfloat16 [65536, 2048], P(('wide', 'narrow'))
- new_gate: bfloat16 [4, 512, 512], P('narrow', 'wide')
- new_up: bfloat16 [4, 512, 512], P('narrow', 'wide')
- new_down: bfloat16 [4, 512, 512], P('narrow', 'wide')
- mom_gate: float32 [4, 512, 512], P('narrow', 'wide')
- mom_up: float32 [4, 512, 512], P('narrow', 'wide')
- mom_down: float32 [4, 512, 512], P('narrow', 'wide')
Inputs may be any that keep to these rules, and one draw needn't show every extreme that they name: `view_lengths`: each row sums to 512; its largest entry is 256.
All inputs are finite; a program needn't handle non-finite values.
Results may differ from a plain program's by a relative error of at most 0.0091.
Values may be sent and summed in bfloat16 or wider, within the bound.
A program may use at most 64 MiB of HBM per device.

v0:
```python
import jax
import jax.numpy as jnp
from jax import lax
from jax.sharding import Mesh
from jax.sharding import PartitionSpec as P

WIDE = ("wide_0", "wide_1", "wide_2")
WIDE_NARROW = ("wide_0", "wide_1", "wide_2", "narrow")


momentum_decay = 0.9
step_size = 0.02
epsilon = 1e-06


def copy_for_each(array, axis):
    size = lax.axis_size(axis)
    return lax.all_to_all(
        jnp.broadcast_to(array[None], (size, *array.shape)), axis, 0, 0, tiled=True
    )


def in_order(parts, dim):
    parts = jnp.moveaxis(parts, 0, dim)
    shape = parts.shape
    return parts.reshape(*shape[:dim], shape[dim] * shape[dim + 1], *shape[dim + 2 :])


def whole_of(array, axes, dim):
    far, near = axes
    parts = copy_for_each(copy_for_each(array, far), near)
    return in_order(parts.swapaxes(0, 1).reshape(-1, *array.shape), dim)


def in_one_piece(arrays, axis, dim, along):
    widths = [a.shape[along] for a in arrays]
    both = jnp.concatenate(arrays, axis=along)
    out = whole_of(both, axis, dim)
    return tuple(jnp.split(out, [sum(widths[:k]) for k in range(1, len(widths))], axis=along))


def filled_up(lines, size):
    spare = -lines.shape[0] % size
    if not spare:
        return lines
    return jnp.concatenate([lines, jnp.zeros((spare, *lines.shape[1:]), lines.dtype)])


def in_blocks(array, dim, size):
    shape = array.shape
    parts = array.reshape(*shape[:dim], size, shape[dim] // size, *shape[dim + 1 :])
    return jnp.moveaxis(parts, dim, 0)


def sent_and_summed(array, axis, dim):
    size = lax.axis_size(axis)
    parts = lax.all_to_all(in_blocks(array, dim, size), axis, 0, 0, tiled=True)
    return jnp.sum(parts.astype(jnp.float32), axis=0)


def summed_rows(array, axes, dim):
    far, near = axes
    own = sent_and_summed(in_blocks(array, dim, lax.axis_size(far)), near, dim + 1)
    return jnp.sum(
        lax.all_to_all(own.astype(jnp.bfloat16), far, 0, 0, tiled=True).astype(jnp.float32), axis=0
    )


def total_of(array, axes):
    lines = array.reshape(-1, array.shape[-1])
    padded = filled_up(lines, lax.axis_size(axes[0]) * lax.axis_size(axes[1]))
    whole = whole_of(summed_rows(padded, axes, 0).astype(jnp.bfloat16), axes, 0)
    return lax.slice_in_dim(whole, 0, len(lines)).reshape(array.shape).astype(jnp.float32)


def for_sending(array):

    def short(part):
        return part.astype(jnp.bfloat16) if part.dtype == jnp.float32 else part

    return jax.tree.map(short, array)


def attend(query_rows, key_rows, value_rows, query_ids, key_ids):
    scaling = query_rows.shape[-1] ** (-0.5)
    scores = (
        jnp.einsum("rhd,ghd->hrg", query_rows, key_rows, preferred_element_type=jnp.float32)
        * scaling
    )
    allowed = query_ids[:, None] == key_ids[None, :]
    scores = jnp.where(allowed[None], scores, -1e30)
    highest = jnp.max(scores, axis=-1, keepdims=True)
    expo = jnp.exp(scores - highest)
    probs = (expo / jnp.sum(expo, axis=-1, keepdims=True)).astype(jnp.bfloat16)
    return jnp.einsum("hrg,ghd->rhd", probs, value_rows, preferred_element_type=jnp.float32)


def rms_gain(field, gains):
    return field * lax.rsqrt(jnp.mean(field * field, axis=-1, keepdims=True) + epsilon) * gains


def silu_slope(pre):
    sig = jax.nn.sigmoid(pre)
    return sig * (1.0 + pre * (1.0 - sig))


def block_gradients(key_rows, value_rows, gate_full, up_full, down_full):
    pre_gate = jnp.dot(key_rows, gate_full, preferred_element_type=jnp.float32)
    pre_up = jnp.dot(key_rows, up_full, preferred_element_type=jnp.float32)
    activ = jax.nn.silu(pre_gate)
    hidden = (activ * pre_up).astype(jnp.bfloat16)
    d_hidden = -lax.dot_general(
        value_rows, down_full, (((1,), (1,)), ((), ())), preferred_element_type=jnp.float32
    )
    d_gate = (d_hidden * pre_up * silu_slope(pre_gate)).astype(jnp.bfloat16)
    d_up = (d_hidden * activ).astype(jnp.bfloat16)
    contract = (((0,), (0,)), ((), ()))
    grad_gate = lax.dot_general(key_rows, d_gate, contract, preferred_element_type=jnp.float32)
    grad_up = lax.dot_general(key_rows, d_up, contract, preferred_element_type=jnp.float32)
    grad_down = -lax.dot_general(hidden, value_rows, contract, preferred_element_type=jnp.float32)
    return (grad_gate, grad_up, grad_down)


def gradients(key_rows, value_rows, gate_full, up_full, down_full):
    row_total, head_size = key_rows.shape
    block = min(row_total, 512)

    def add_block(number, totals):
        start = number * block
        terms = block_gradients(key_rows, value_rows, gate_full, up_full, down_full)
        return tuple((total + term for total, term in zip(totals, terms)))

    zeros = jnp.zeros((head_size, head_size), jnp.float32)
    return lax.fori_loop(0, row_total // block, add_block, (zeros, zeros, zeros))


def renormed(weight, moment, radius):
    old = weight.astype(jnp.float32)
    moved = old - step_size * moment / radius
    ratio = jnp.sqrt(jnp.sum(old * old, axis=-1, keepdims=True) + epsilon) / jnp.sqrt(
        jnp.sum(moved * moved, axis=-1, keepdims=True) + epsilon
    )
    return (moved * ratio).astype(jnp.bfloat16)


def apply_fast(query_rows, gate_full, up_full, down_full, gains):
    row_total, width = query_rows.shape
    block = min(row_total, 512)

    def one_block(block_rows):
        pre_gate = jnp.dot(block_rows, gate_full, preferred_element_type=jnp.float32)
        pre_up = jnp.dot(block_rows, up_full, preferred_element_type=jnp.float32)
        hidden = (jax.nn.silu(pre_gate) * pre_up).astype(jnp.bfloat16)
        fast_raw = jnp.dot(hidden, down_full, preferred_element_type=jnp.float32)
        return rms_gain(fast_raw, gains).astype(jnp.bfloat16)

    return lax.map(one_block, query_rows.reshape(row_total // block, block, width)).reshape(
        row_total, width
    )


def fast_branch(query_rows, key_rows, value_rows, gains, weights, moments):
    gate_full, up_full, down_full = in_one_piece(
        (weights[0], weights[1], weights[2]), (("wide_0", "wide_1"), "wide_2"), 0, 1
    )
    grads = gradients(key_rows, value_rows, gate_full, up_full, down_full)
    wide_size = lax.axis_size(WIDE)
    grad_scale = float(key_rows.shape[0] * wide_size) ** (-0.5)
    head_size = key_rows.shape[1]
    row_count = weights[0].shape[0]
    offset = lax.axis_index(WIDE) * row_count
    blank = jnp.zeros((head_size, head_size), jnp.float32)
    placed = tuple(
        (
            lax.dynamic_update_slice_in_dim(blank, momentum_decay * moment, offset, 0)
            + part * grad_scale
            for moment, part in zip(moments, grads)
        )
    )
    full_moments = jax.tree.map(
        lambda part: total_of(part, (("wide_0", "wide_1"), "wide_2")), for_sending(placed)
    )
    full_new = tuple(
        (
            renormed(weight, moment, jnp.sqrt(jnp.mean(moment * moment) + epsilon))
            for weight, moment in zip((gate_full, up_full, down_full), full_moments)
        )
    )
    fresh = tuple((lax.dynamic_slice_in_dim(weight, offset, row_count, 0) for weight in full_new))
    moment_new = tuple(
        (lax.dynamic_slice_in_dim(moment, offset, row_count, 0) for moment in full_moments)
    )
    fast_out = apply_fast(query_rows, full_new[0], full_new[1], full_new[2], gains)
    return (fast_out, fresh, moment_new)


def per_device(
    queries, keys, values, view_lengths, gain, w_gate, w_up, w_down, m_gate, m_up, m_down
):
    narrow_size = lax.axis_size("narrow")
    narrow_index = lax.axis_index("narrow")
    tok_dev = queries.shape[0]
    group_size = tok_dev * narrow_size
    head_size = queries.shape[1] // narrow_size
    ends = jnp.cumsum(view_lengths[0])
    position = jnp.arange(group_size, dtype=jnp.int32)
    view_ids = jnp.sum((position[:, None] >= ends[None, :-1]).astype(jnp.int32), axis=1)
    head_gains = lax.dynamic_slice_in_dim(gain, narrow_index * head_size, head_size, 0)
    weights = (w_gate[0], w_up[0], w_down[0])
    moments = (m_gate[0], m_up[0], m_down[0])
    query_head, key_head, value_head = (
        lax.all_to_all(queries, "narrow", split_axis=1, concat_axis=0, tiled=True),
        lax.all_to_all(keys, "narrow", split_axis=1, concat_axis=0, tiled=True),
        lax.all_to_all(values, "narrow", split_axis=1, concat_axis=0, tiled=True),
    )
    attn = attend(query_head[:, None], key_head[:, None], value_head[:, None], view_ids, view_ids)
    view_head = rms_gain(attn[:, 0], head_gains).astype(jnp.bfloat16)
    fast_out, fresh, moment_new = fast_branch(
        query_head, key_head, value_head, head_gains, weights, moments
    )
    view_out, fast_tokens = (
        lax.all_to_all(view_head, "narrow", split_axis=0, concat_axis=1, tiled=True),
        lax.all_to_all(fast_out, "narrow", split_axis=0, concat_axis=1, tiled=True),
    )
    output = (view_out.astype(jnp.float32) + fast_tokens.astype(jnp.float32)).astype(jnp.bfloat16)
    return (
        output,
        fresh[0][None],
        fresh[1][None],
        fresh[2][None],
        moment_new[0][None],
        moment_new[1][None],
        moment_new[2][None],
    )


def solution(mesh):
    split = Mesh(
        mesh.devices.reshape(4, 16, 2, mesh.shape["narrow"]),
        ("wide_0", "wide_1", "wide_2", "narrow"),
    )
    in_specs = (
        P(WIDE_NARROW, None),
        P(WIDE_NARROW, None),
        P(WIDE_NARROW, None),
        P(WIDE, None),
        P(),
        P("narrow", WIDE, None),
        P("narrow", WIDE, None),
        P("narrow", WIDE, None),
        P("narrow", WIDE, None),
        P("narrow", WIDE, None),
        P("narrow", WIDE, None),
    )
    out_specs = (
        P(WIDE_NARROW, None),
        P("narrow", WIDE, None),
        P("narrow", WIDE, None),
        P("narrow", WIDE, None),
        P("narrow", WIDE, None),
        P("narrow", WIDE, None),
        P("narrow", WIDE, None),
    )
    return jax.shard_map(
        per_device, mesh=split, in_specs=in_specs, out_specs=out_specs, check_vma=False
    )
```

profile of v0, /device:TPU:1, one launch (start us, length us, event | category | flops | bytes accessed | tf_op | source)
XLA Modules:
  0.0 358.0 jit_solution(6512135417536922821)
XLA Ops:
  2.7 5.1 %all-to-all-start.2 = ((bf16[128,4,512]{0,2,1:T(8,128)(2,1)}), bf16[128,4,512]{0,2,1:T(8,128)(2,1)S(1)}, u32[]{:S(2)}, u32[]{:S(2)}) async-start(bf16[128,4,512]{0,2,1:T(8,128)(2,1)} %bitcast.8), calls=%async_computation.2 | async-start | bytes 1048576 | tf_op jit(solution)/shard_map/all_to_all | solution.py:214
  8.9 5.9 %all-to-all-done.2 = bf16[128,4,512]{0,2,1:T(8,128)(2,1)S(1)} async-done(((bf16[128,4,512]{0,2,1:T(8,128)(2,1)}), bf16[128,4,512]{0,2,1:T(8,128)(2,1)S(1)}, u32[]{:S(2)}, u32[]{:S(2)}) %all-to-all-start.2) | async-done | bytes 524320 | tf_op jit(solution)/shard_map/all_to_all | solution.py:214
  18.5 6.8 %all-to-all-done.1 = bf16[128,4,512]{0,2,1:T(8,128)(2,1)S(1)} async-done(((bf16[128,4,512]{0,2,1:T(8,128)(2,1)}), bf16[128,4,512]{0,2,1:T(8,128)(2,1)S(1)}, u32[]{:S(2)}, u32[]{:S(2)}) %all-to-all-start.1) | async-done | bytes 524320 | tf_op jit(solution)/shard_map/all_to_all | solution.py:213
  26.4 19.9 %all-to-all-start.4 = ((bf16[64,4,1536]{2,1,0:T(4,128)(2,1)}), bf16[64,4,1536]{2,1,0:T(4,128)(2,1)S(1)}, u32[]{:S(2)}, u32[]{:S(2)}) async-start(bf16[64,4,1536]{2,1,0:T(4,128)(2,1)} %broadcast_in_dim.37), calls=%async_computation.4 | async-start | bytes 1572864 | tf_op jit(solution)/shard_map/all_to_all | solution.py:18
  50.4 33.1 %all-to-all-done.4 = bf16[64,4,1536]{2,1,0:T(4,128)(2,1)S(1)} async-done(((bf16[64,4,1536]{2,1,0:T(4,128)(2,1)}), bf16[64,4,1536]{2,1,0:T(4,128)(2,1)S(1)}, u32[]{:S(2)}, u32[]{:S(2)}) %all-to-all-start.4) | async-done | bytes 786464 | tf_op jit(solution)/shard_map/all_to_all | solution.py:18
  83.9 10.5 %all_to_all.141 = bf16[2,64,4,1536]{3,2,1,0:T(4,128)(2,1)S(1)} all-to-all(bf16[2,64,4,1536]{3,2,1,0:T(4,128)(2,1)S(1)} %broadcast_in_dim.38), channel_id=1, replica_groups=mesh['wide_0'=4,'wide_1'=16,'wide_2'=2,'narrow'=4] {'wide_2'}, dimensions={0} | all-to-all | bytes 3145728 | tf_op jit(solution)/shard_map/all_to_all | solution.py:18
  107.5 4.6 %all_to_all.142 = bf16[2,64,4,512]{3,2,1,0:T(4,128)(2,1)} all-to-all(bf16[2,64,4,512]{3,2,1,0:T(4,128)(2,1)S(1)} %copy.160), channel_id=1, replica_groups=mesh['wide_0'=4,'wide_1'=16,'wide_2'=2,'narrow'=4] {'wide_2'}, dimensions={0} | all-to-all | bytes 1048576 | tf_op jit(solution)/shard_map/all_to_all | solution.py:57
  131.3 5.7 %all_to_all.143 = bf16[2,64,4,512]{3,2,1,0:T(4,128)(2,1)} all-to-all(bf16[2,64,4,512]{3,2,1,0:T(4,128)(2,1)} %copy.154), channel_id=1, replica_groups=mesh['wide_0'=4,'wide_1'=16,'wide_2'=2,'narrow'=4] {'wide_2'}, dimensions={0} | all-to-all | bytes 1048576 | tf_op jit(solution)/shard_map/all_to_all | solution.py:57
  137.0 5.2 %all_to_all.144 = bf16[2,64,4,512]{3,2,1,0:T(4,128)(2,1)S(1)} all-to-all(bf16[2,64,4,512]{3,2,1,0:T(4,128)(2,1)} %copy.150), channel_id=1, replica_groups=mesh['wide_0'=4,'wide_1'=16,'wide_2'=2,'narrow'=4] {'wide_2'}, dimensions={0} | all-to-all | bytes 1048576 | tf_op jit(solution)/shard_map/all_to_all | solution.py:57
  142.2 7.7 %all-to-all-start.15 = ((bf16[64,4,512]{2,1,0:T(4,128)(2,1)}), bf16[64,4,512]{2,1,0:T(4,128)(2,1)S(1)}, u32[]{:S(2)}, u32[]{:S(2)}) async-start(bf16[64,4,512]{2,1,0:T(4,128)(2,1)} %reduce_sum.203), calls=%async_computation.15 | async-start | bytes 524288 | tf_op jit(solution)/shard_map/all_to_all | solution.py:65
  152.0 17.7 %all-to-all-done.15 = bf16[64,4,512]{2,1,0:T(4,128)(2,1)S(1)} async-done(((bf16[64,4,512]{2,1,0:T(4,128)(2,1)}), bf16[64,4,512]{2,1,0:T(4,128)(2,1)S(1)}, u32[]{:S(2)}, u32[]{:S(2)}) %all-to-all-start.15) | async-done | bytes 262176 | tf_op jit(solution)/shard_map/all_to_all | solution.py:65
  170.5 7.1 %all-to-all-start.11 = ((bf16[64,4,512]{2,1,0:T(4,128)(2,1)}), bf16[64,4,512]{2,1,0:T(4,128)(2,1)S(1)}, u32[]{:S(2)}, u32[]{:S(2)}) async-start(bf16[64,4,512]{2,1,0:T(4,128)(2,1)} %reduce_sum.198), calls=%async_computation.11 | async-start | bytes 524288 | tf_op jit(solution)/shard_map/all_to_all | solution.py:65
  178.8 17.5 %all-to-all-done.11 = bf16[64,4,512]{2,1,0:T(4,128)(2,1)S(1)} async-done(((bf16[64,4,512]{2,1,0:T(4,128)(2,1)}), bf16[64,4,512]{2,1,0:T(4,128)(2,1)S(1)}, u32[]{:S(2)}, u32[]{:S(2)}) %all-to-all-start.11) | async-done | bytes 262176 | tf_op jit(solution)/shard_map/all_to_all | solution.py:65
  196.3 7.5 %all-to-all-start.7 = ((bf16[64,4,512]{2,1,0:T(4,128)(2,1)}), bf16[64,4,512]{2,1,0:T(4,128)(2,1)S(1)}, u32[]{:S(2)}, u32[]{:S(2)}) async-start(bf16[64,4,512]{2,1,0:T(4,128)(2,1)} %reduce_sum.193), calls=%async_computation.7 | async-start | bytes 524288 | tf_op jit(solution)/shard_map/all_to_all | solution.py:65
  204.9 17.0 %all-to-all-done.7 = bf16[64,4,512]{2,1,0:T(4,128)(2,1)S(1)} async-done(((bf16[64,4,512]{2,1,0:T(4,128)(2,1)}), bf16[64,4,512]{2,1,0:T(4,128)(2,1)S(1)}, u32[]{:S(2)}, u32[]{:S(2)}) %all-to-all-start.7) | async-done | bytes 262176 | tf_op jit(solution)/shard_map/all_to_all | solution.py:65
  222.7 7.9 %all-to-all-start.16 = ((bf16[64,4,512]{2,1,0:T(4,128)(2,1)}), bf16[64,4,512]{2,1,0:T(4,128)(2,1)S(1)}, u32[]{:S(2)}, u32[]{:S(2)}) async-start(bf16[64,4,512]{2,1,0:T(4,128)(2,1)} %broadcast_in_dim.43), calls=%async_computation.16 | async-start | bytes 524288 | tf_op jit(solution)/shard_map/all_to_all | solution.py:18
  231.7 16.8 %all-to-all-done.16 = bf16[64,4,512]{2,1,0:T(4,128)(2,1)S(1)} async-done(((bf16[64,4,512]{2,1,0:T(4,128)(2,1)}), bf16[64,4,512]{2,1,0:T(4,128)(2,1)S(1)}, u32[]{:S(2)}, u32[]{:S(2)}) %all-to-all-start.16) | async-done | bytes 262176 | tf_op jit(solution)/shard_map/all_to_all | solution.py:18
  248.6 7.8 %all_to_all.145 = bf16[2,64,4,512]{3,2,1,0:T(4,128)(2,1)S(1)} all-to-all(bf16[2,64,4,512]{3,2,1,0:T(4,128)(2,1)S(1)} %broadcast_in_dim.44), channel_id=1, replica_groups=mesh['wide_0'=4,'wide_1'=16,'wide_2'=2,'narrow'=4] {'wide_2'}, dimensions={0} | all-to-all | bytes 1048576 | tf_op jit(solution)/shard_map/all_to_all | solution.py:18
  257.2 6.2 %all-to-all-start.12 = ((bf16[64,4,512]{2,1,0:T(4,128)(2,1)}), bf16[64,4,512]{2,1,0:T(4,128)(2,1)S(1)}, u32[]{:S(2)}, u32[]{:S(2)}) async-start(bf16[64,4,512]{2,1,0:T(4,128)(2,1)} %broadcast_in_dim.41), calls=%async_computation.12 | async-start | bytes 524288 | tf_op jit(solution)/shard_map/all_to_all | solution.py:18
  268.0 15.3 %all-to-all-done.12 = bf16[64,4,512]{2,1,0:T(4,128)(2,1)S(1)} async-done(((bf16[64,4,512]{2,1,0:T(4,128)(2,1)}), bf16[64,4,512]{2,1,0:T(4,128)(2,1)S(1)}, u32[]{:S(2)}, u32[]{:S(2)}) %all-to-all-start.12) | async-done | bytes 262176 | tf_op jit(solution)/shard_map/all_to_all | solution.py:18
  283.5 5.8 %all_to_all.146 = bf16[2,64,4,512]{3,2,1,0:T(4,128)(2,1)S(1)} all-to-all(bf16[2,64,4,512]{3,2,1,0:T(4,128)(2,1)S(1)} %broadcast_in_dim.42), channel_id=1, replica_groups=mesh['wide_0'=4,'wide_1'=16,'wide_2'=2,'narrow'=4] {'wide_2'}, dimensions={0} | all-to-all | bytes 1048576 | tf_op jit(solution)/shard_map/all_to_all | solution.py:18
  290.1 6.2 %all-to-all-start.8 = ((bf16[64,4,512]{2,1,0:T(4,128)(2,1)}), bf16[64,4,512]{2,1,0:T(4,128)(2,1)S(1)}, u32[]{:S(2)}, u32[]{:S(2)}) async-start(bf16[64,4,512]{2,1,0:T(4,128)(2,1)} %broadcast_in_dim.39), calls=%async_computation.8 | async-start | bytes 524288 | tf_op jit(solution)/shard_map/all_to_all | solution.py:18
  308.9 7.2 %all-to-all-done.8 = bf16[64,4,512]{2,1,0:T(4,128)(2,1)S(1)} async-done(((bf16[64,4,512]{2,1,0:T(4,128)(2,1)}), bf16[64,4,512]{2,1,0:T(4,128)(2,1)S(1)}, u32[]{:S(2)}, u32[]{:S(2)}) %all-to-all-start.8) | async-done | bytes 262176 | tf_op jit(solution)/shard_map/all_to_all | solution.py:18
  316.3 5.8 %all_to_all.147 = bf16[2,64,4,512]{3,2,1,0:T(4,128)(2,1)S(1)} all-to-all(bf16[2,64,4,512]{3,2,1,0:T(4,128)(2,1)S(1)} %broadcast_in_dim.40), channel_id=1, replica_groups=mesh['wide_0'=4,'wide_1'=16,'wide_2'=2,'narrow'=4] {'wide_2'}, dimensions={0} | all-to-all | bytes 1048576 | tf_op jit(solution)/shard_map/all_to_all | solution.py:18
  (142 shorter events, 104.2 us)
Async XLA Ops:
  0.6 7.2 %copy-start.16 = (bf16[128,2048]{1,0:T(8,128)(2,1)S(1)}, bf16[128,2048]{1,0:T(8,128)(2,1)}, u32[]{:S(2)}) copy-start(bf16[128,2048]{1,0:T(8,128)(2,1)} %param.12) | copy-start | bytes 1572868
  2.7 15.7 %copy-start.21 = (bf16[1,4,512]{2,1,0:T(4,128)(2,1)S(1)}, bf16[1,4,512]{2,1,0:T(4,128)(2,1)}, u32[]{:S(2)}) copy-start(bf16[1,4,512]{2,1,0:T(4,128)(2,1)} %param.18) | copy-start | bytes 12292
  2.7 15.7 %copy-start.22 = (bf16[1,4,512]{2,1,0:T(4,128)(2,1)S(1)}, bf16[1,4,512]{2,1,0:T(4,128)(2,1)}, u32[]{:S(2)}) copy-start(bf16[1,4,512]{2,1,0:T(4,128)(2,1)} %param.17) | copy-start | bytes 12292
  2.7 15.7 %copy-start.23 = (bf16[1,4,512]{2,1,0:T(4,128)(2,1)S(1)}, bf16[1,4,512]{2,1,0:T(4,128)(2,1)}, u32[]{:S(2)}) copy-start(bf16[1,4,512]{2,1,0:T(4,128)(2,1)} %param.16) | copy-start | bytes 12292
  2.7 12.1 %all-to-all-start.2 = ((bf16[128,4,512]{0,2,1:T(8,128)(2,1)}), bf16[128,4,512]{0,2,1:T(8,128)(2,1)S(1)}, u32[]{:S(2)}, u32[]{:S(2)}) async-start(bf16[128,4,512]{0,2,1:T(8,128)(2,1)} %bitcast.8), calls=%async_computation.2 | async-start | bytes 1048576 | tf_op jit(solution)/shard_map/all_to_all | solution.py:214
  14.8 31.5 %copy-start.18 = (f32[1,4,512]{2,1,0:T(4,128)S(1)}, f32[1,4,512]{2,1,0:T(4,128)}, u32[]{:S(2)}) copy-start(f32[1,4,512]{2,1,0:T(4,128)} %param.21) | copy-start | bytes 24580
  14.8 10.5 %all-to-all-start.1 = ((bf16[128,4,512]{0,2,1:T(8,128)(2,1)}), bf16[128,4,512]{0,2,1:T(8,128)(2,1)S(1)}, u32[]{:S(2)}, u32[]{:S(2)}) async-start(bf16[128,4,512]{0,2,1:T(8,128)(2,1)} %bitcast.5), calls=%async_computation.1 | async-start | bytes 1048576 | tf_op jit(solution)/shard_map/all_to_all | solution.py:213
  18.4 28.1 %copy-start.19 = (f32[1,4,512]{2,1,0:T(4,128)S(1)}, f32[1,4,512]{2,1,0:T(4,128)}, u32[]{:S(2)}) copy-start(f32[1,4,512]{2,1,0:T(4,128)} %param.19) | copy-start | bytes 24580
  18.4 28.9 %copy-start.17 = (bf16[128,2048]{1,0:T(8,128)(2,1)S(1)}, bf16[128,2048]{1,0:T(8,128)(2,1)}, u32[]{:S(2)}) copy-start(bf16[128,2048]{1,0:T(8,128)(2,1)} %param.11) | copy-start | bytes 1572868
  26.4 57.1 %all-to-all-start.4 = ((bf16[64,4,1536]{2,1,0:T(4,128)(2,1)}), bf16[64,4,1536]{2,1,0:T(4,128)(2,1)S(1)}, u32[]{:S(2)}, u32[]{:S(2)}) async-start(bf16[64,4,1536]{2,1,0:T(4,128)(2,1)} %broadcast_in_dim.37), calls=%async_computation.4 | async-start | bytes 1572864 | tf_op jit(solution)/shard_map/all_to_all | solution.py:18
  112.2 19.1 %all-to-all-start = ((bf16[128,4,512]{0,2,1:T(8,128)(2,1)}), bf16[128,4,512]{0,2,1:T(8,128)(2,1)S(1)}, u32[]{:S(2)}, u32[]{:S(2)}) async-start(bf16[128,4,512]{0,2,1:T(8,128)(2,1)} %bitcast.2), calls=%async_computation | async-start | bytes 1048576 | tf_op jit(solution)/shard_map/all_to_all | solution.py:212
  118.5 3.1 copy-start.14
  126.0 4.1 %copy-start.3 = (bf16[2,64,4,512]{3,2,1,0:T(4,128)(2,1)S(1)}, bf16[2,64,4,512]{3,2,1,0:T(4,128)(2,1)}, u32[]{:S(2)}) copy-start(bf16[2,64,4,512]{3,2,1,0:T(4,128)(2,1)} %all_to_all.142) | copy-start | bytes 1572868
  142.2 27.5 %all-to-all-start.15 = ((bf16[64,4,512]{2,1,0:T(4,128)(2,1)}), bf16[64,4,512]{2,1,0:T(4,128)(2,1)S(1)}, u32[]{:S(2)}, u32[]{:S(2)}) async-start(bf16[64,4,512]{2,1,0:T(4,128)(2,1)} %reduce_sum.203), calls=%async_computation.15 | async-start | bytes 524288 | tf_op jit(solution)/shard_map/all_to_all | solution.py:65
  152.0 78.6 %copy-start.24 = (s32[1,4]{1,0:T(1,128)S(1)}, s32[1,4]{1,0:T(1,128)}, u32[]{:S(2)}) copy-start(s32[1,4]{1,0:T(1,128)} %param.14) | copy-start | bytes 52
  170.5 25.8 %all-to-all-start.11 = ((bf16[64,4,512]{2,1,0:T(4,128)(2,1)}), bf16[64,4,512]{2,1,0:T(4,128)(2,1)S(1)}, u32[]{:S(2)}, u32[]{:S(2)}) async-start(bf16[64,4,512]{2,1,0:T(4,128)(2,1)} %reduce_sum.198), calls=%async_computation.11 | async-start | bytes 524288 | tf_op jit(solution)/shard_map/all_to_all | solution.py:65
  196.3 25.6 %all-to-all-start.7 = ((bf16[64,4,512]{2,1,0:T(4,128)(2,1)}), bf16[64,4,512]{2,1,0:T(4,128)(2,1)S(1)}, u32[]{:S(2)}, u32[]{:S(2)}) async-start(bf16[64,4,512]{2,1,0:T(4,128)(2,1)} %reduce_sum.193), calls=%async_computation.7 | async-start | bytes 524288 | tf_op jit(solution)/shard_map/all_to_all | solution.py:65
  222.7 25.8 %all-to-all-start.16 = ((bf16[64,4,512]{2,1,0:T(4,128)(2,1)}), bf16[64,4,512]{2,1,0:T(4,128)(2,1)S(1)}, u32[]{:S(2)}, u32[]{:S(2)}) async-start(bf16[64,4,512]{2,1,0:T(4,128)(2,1)} %broadcast_in_dim.43), calls=%async_computation.16 | async-start | bytes 524288 | tf_op jit(solution)/shard_map/all_to_all | solution.py:18
  257.2 26.1 %all-to-all-start.12 = ((bf16[64,4,512]{2,1,0:T(4,128)(2,1)}), bf16[64,4,512]{2,1,0:T(4,128)(2,1)S(1)}, u32[]{:S(2)}, u32[]{:S(2)}) async-start(bf16[64,4,512]{2,1,0:T(4,128)(2,1)} %broadcast_in_dim.41), calls=%async_computation.12 | async-start | bytes 524288 | tf_op jit(solution)/shard_map/all_to_all | solution.py:18
  290.1 26.1 %all-to-all-start.8 = ((bf16[64,4,512]{2,1,0:T(4,128)(2,1)}), bf16[64,4,512]{2,1,0:T(4,128)(2,1)S(1)}, u32[]{:S(2)}, u32[]{:S(2)}) async-start(bf16[64,4,512]{2,1,0:T(4,128)(2,1)} %broadcast_in_dim.39), calls=%async_computation.8 | async-start | bytes 524288 | tf_op jit(solution)/shard_map/all_to_all | solution.py:18
  322.1 21.3 %all-to-all-start.3 = ((bf16[4,128,512]{2,1,0:T(8,128)(2,1)}), bf16[4,128,512]{2,1,0:T(8,128)(2,1)}, u32[]{:S(2)}, u32[]{:S(2)}) async-start(bf16[4,128,512]{2,1,0:T(8,128)(2,1)} %multiply_convert_fusion.7), calls=%async_computation.3 | async-start | bytes 1048576 | tf_op jit(solution)/shard_map/all_to_all | solution.py:222
  332.3 2.6 copy-start
  332.3 2.7 copy-start.1
  343.4 12.6 %all-to-all-start.18 = ((bf16[4,128,512]{2,1,0:T(8,128)(2,1)}), bf16[4,128,512]{2,1,0:T(8,128)(2,1)S(1)}, u32[]{:S(2)}, u32[]{:S(2)}) async-start(bf16[4,128,512]{2,1,0:T(8,128)(2,1)} %bitcast.38), calls=%async_computation.18 | async-start | bytes 1048576 | tf_op jit(solution)/shard_map/all_to_all | solution.py:223
  (13 other events, 18.0 us)
where the time goes:
time: 361 us; the launch traced here: 358 us
  waiting for transfers between devices  141 us (39%)
  starting transfers between devices  83.6 us (23%)
  local copies, waits for them, and re-layouts  47.5 us (13%)
  blocking collectives  45.5 us (13%)
  other arithmetic  23.3 us (6%)
  matrix products  13.9 us (4%)
    all_to_all x4, waiting for transfers between devices, copy_for_each(): lax.all_to_all(jnp.broadcast_to(array[None], (size, *array.shape)), axis,...  72.4 us
    all_to_all x3, waiting for transfers between devices, summed_rows(): lax.all_to_all(own.astype(jnp.bfloat16), far, 0, 0, tiled=True)  52.2 us
    all_to_all x4, starting transfers between devices, copy_for_each(): lax.all_to_all(jnp.broadcast_to(array[None], (size, *array.shape)), axis,...  40.3 us
    all_to_all x4, blocking collectives, copy_for_each(): lax.all_to_all(jnp.broadcast_to(array[None], (size, *array.shape)), axis,...  30 us
    all_to_all x3, starting transfers between devices, summed_rows(): lax.all_to_all(own.astype(jnp.bfloat16), far, 0, 0, tiled=True)  22.3 us
    all_to_all x3, blocking collectives, sent_and_summed(): parts = lax.all_to_all(in_blocks(array, dim, size), axis, 0, 0, tiled=True)  15.5 us
    convert_element_type x6, local copies, waits for them, and re-layouts, total_of(): lax.slice_in_dim(whole, 0, len(lines)).reshape(array.shape)  10.2 us
    unnamed x56, local copies, waits for them, and re-layouts  8.1 us
  transfers between devices with their start and end apart: 12, of which 10 were waited for; matrix products, arithmetic and copies ran while one was open for 17% of the time, Pallas kernels for 0%

commit v1 on v0

v1 whole, which is shorter than its diff:
```python
import functools

import jax
import jax.numpy as jnp
from jax import lax
from jax.experimental import pallas as pl
from jax.experimental.pallas import tpu as pltpu
from jax.sharding import Mesh
from jax.sharding import PartitionSpec as P

WIDE = ("wide_0", "wide_1", "wide_2")
WIDE_NARROW = ("wide_0", "wide_1", "wide_2", "narrow")
MESH = pl.DeviceIdType.MESH

momentum_decay = 0.9
step_size = 0.02
epsilon = 1e-06

NX, NZ, NY = 4, 16, 4
HEAD = 512
HALF = 256
GROUP = 512
TOK = 128
CHIPS = NX * NZ
TOKENS = 65536
F32 = jnp.float32
BF16 = jnp.bfloat16


def nt(a, b):
    return lax.dot_general(a, b, (((1,), (1,)), ((), ())), preferred_element_type=F32)


def mm(a, b):
    return jnp.dot(a, b, preferred_element_type=F32)


def rms(field, gains):
    return field * lax.rsqrt(jnp.mean(field * field, axis=-1, keepdims=True) + epsilon) * gains


def remote(src, dst, send, recv, **where):
    return pltpu.make_async_remote_copy(
        src_ref=src, dst_ref=dst, send_sem=send, recv_sem=recv, device_id=where, device_id_type=MESH
    )


def loop(n, body, start=0):
    def step(i, carry):
        body(i)
        return carry

    lax.fori_loop(start, n, step, 0)


def kernel(
    q_in, k_in, v_in, lengths, gain, wg, wu, wd, mg, mu, md,
    out, ng, nu, nd, og, ou, od,
    qh, kh, vh, kt, ht, hid, dg, du, ex, exr, mhalf, wbuf, w2, own, gsend, grecv,
    xs, xr, zs, zr, mbuf, n2, view, oblk,
    tok_send, tok_recv, tok_own, ex_sem, wz_s, wz_r, wx_s, wx_r, wc_s, wc_r,
    mz_s, mz_r, mx_s, mx_r, mc_s, mc_r, gs_s, gs_r, rx_s, rx_r, rz_s, rz_r, o_s, o_r, o_own,
):
    x = lax.axis_index("wide_0")
    z = lax.axis_index("wide_1")
    c = lax.axis_index("wide_2")
    y = lax.axis_index("narrow")
    chip = x * NZ + z
    other = 1 - c

    for t, w in enumerate((wg, wu, wd)):
        ex[t] = w[0].astype(F32)
    for t, m in enumerate((mg, mu, md)):
        ex[3 + t] = m[0]

    barrier = pltpu.get_barrier_semaphore()
    pl.semaphore_signal(barrier, inc=1, device_id={"wide_2": other}, device_id_type=MESH)
    for d in range(1, NY):
        pl.semaphore_signal(
            barrier, inc=1, device_id={"narrow": lax.rem(y + d, NY)}, device_id_type=MESH
        )
    for d in range(1, NX):
        pl.semaphore_signal(
            barrier, inc=1, device_id={"wide_0": lax.rem(x + d, NX)}, device_id_type=MESH
        )

    def greet(d):
        pl.semaphore_signal(
            barrier, inc=1, device_id={"wide_1": lax.rem(z + d, NZ)}, device_id_type=MESH
        )

    loop(NZ, greet, 1)
    pl.semaphore_wait(barrier, NY - 1 + NX - 1 + NZ - 1 + 1)

    def cols(who):
        return pl.ds(pl.multiple_of(who * HEAD, HEAD), HEAD)

    def rows(who):
        return pl.ds(pl.multiple_of(who * TOK, TOK), TOK)

    trio = ((k_in, kh), (v_in, vh), (q_in, qh))

    def tok_copy(t, d):
        src, dst = trio[t]
        to = lax.rem(y + d, NY)
        return remote(
            src.at[:, cols(to)], dst.at[rows(y)], tok_send.at[t, d], tok_recv.at[t, d], narrow=to
        )

    def tok_wait(t):
        src, dst = trio[t]
        for d in range(1, NY):
            frm = lax.rem(y + NY - d, NY)
            remote(
                src.at[:, cols(y)], dst.at[rows(frm)], tok_send.at[t, d], tok_recv.at[t, d], narrow=frm
            ).wait_recv()
        tok_local(t).wait()

    def tok_local(t):
        src, dst = trio[t]
        return pltpu.make_async_copy(src.at[:, cols(y)], dst.at[rows(y)], tok_own.at[t])

    swap = remote(ex, exr, ex_sem.at[0], ex_sem.at[1], wide_2=other)
    swap.start()
    for t in range(3):
        for d in (1, 3, 2):
            tok_copy(t, d).start()
        tok_local(t).start()

    def z_copy(buf, s, r, d):
        return remote(
            buf.at[chip, c], buf.at[chip, c], s.at[d], r.at[d], wide_1=lax.rem(z + d, NZ)
        )

    def block_of(d):
        return x * NZ + lax.rem(z + NZ - d, NZ)

    def x_copy(buf, s, r, e, d):
        b = block_of(d)
        return remote(
            buf.at[b, c], buf.at[b, c], s.at[e, d], r.at[e, d], wide_0=lax.rem(x + e, NX)
        )

    def c_copy(buf, s, r, e):
        first = pl.multiple_of(lax.rem(x + NX - e, NX) * NZ, NZ)
        part = buf.at[pl.ds(first, NZ), c]
        return remote(part, part, s.at[e], r.at[e], wide_2=other)

    def gather(buf, z_s, z_r, x_s, x_r, c_s, c_r):
        for d in range(1, NZ // 2):
            z_copy(buf, z_s, z_r, d).start()
            z_copy(buf, z_s, z_r, NZ - d).start()
        z_copy(buf, z_s, z_r, NZ // 2).start()

        def forward(d):
            for e in (1, 3, 2):
                x_copy(buf, x_s, x_r, e, d).start()

        forward(0)

        def relay(d):
            b = block_of(d)
            remote(buf.at[b, c], buf.at[b, c], z_s.at[d], z_r.at[d], wide_1=z).wait_recv()
            forward(d)

        def relay_pair(d):
            relay(d)
            relay(NZ - d)

        loop(NZ // 2, relay_pair, 1)
        relay(NZ // 2)
        c_copy(buf, c_s, c_r, 0).start()
        for e in (1, 3, 2):

            def landed(d, e=e):
                b = lax.rem(x + NX - e, NX) * NZ + lax.rem(z + NZ - d, NZ)
                remote(
                    buf.at[b, c], buf.at[b, c], x_s.at[e, d], x_r.at[e, d], wide_0=x
                ).wait_recv()

            loop(NZ, landed)
            c_copy(buf, c_s, c_r, e).start()
        for e in range(NX):
            first = pl.multiple_of(lax.rem(x + NX - e, NX) * NZ, NZ)
            part = buf.at[pl.ds(first, NZ), other]
            remote(part, part, c_s.at[e], c_r.at[e], wide_2=other).wait_recv()

    def gather_sent(buf, z_s, z_r, x_s, x_r, c_s, c_r):
        def far(d):
            z_copy(buf, z_s, z_r, d).wait_send()

        loop(NZ, far, 1)

        def near(d):
            for e in range(1, NX):
                x_copy(buf, x_s, x_r, e, d).wait_send()

        loop(NZ, near)
        for e in range(NX):
            c_copy(buf, c_s, c_r, e).wait_send()

    swap.wait_recv()
    mine, theirs = ex[...], exr[...]
    first = c == 0
    rows8 = jnp.concatenate(
        [jnp.where(first, mine, theirs), jnp.where(first, theirs, mine)], axis=1
    )
    half = jnp.where(first, rows8[:, :, :HALF], rows8[:, :, HALF:])
    wbuf[chip, c] = half[:3].astype(BF16)
    mhalf[...] = half[3:]
    gather(wbuf, wz_s, wz_r, wx_s, wx_r, wc_s, wc_r)

    def square(i):
        r = pl.ds(pl.multiple_of(i * TOK, TOK), TOK)
        b = pl.ds(pl.multiple_of(i * NZ, NZ), NZ)
        for t in range(3):
            for h in range(2):
                part = wbuf[b, h, t].astype(F32).reshape(TOK, HALF)
                w2[t, r, h * HALF : (h + 1) * HALF] = part.astype(BF16)

    loop(4, square)
    tok_wait(0)
    tok_wait(1)

    kt[...] = kh[...].T

    def back(i):
        r = pl.ds(pl.multiple_of(i * TOK, TOK), TOK)
        kb = kh[r]
        pre_gate = mm(kb, w2[0])
        pre_up = mm(kb, w2[1])
        d_hidden = -nt(vh[r], w2[2])
        sig = jax.nn.sigmoid(pre_gate)
        activ = pre_gate * sig
        hid[r] = (activ * pre_up).astype(BF16)
        dg[r] = (d_hidden * pre_up * (sig * (1.0 + pre_gate * (1.0 - sig)))).astype(BF16)
        du[r] = (d_hidden * activ).astype(BF16)

    loop(4, back)
    ht[...] = hid[...].T

    def g_copy(b):
        return remote(gsend.at[b], grecv.at[b], gs_s.at[b], gs_r.at[b], wide_2=other)

    def grad(i):
        b = lax.rem(x + 1 + i, NX)
        r = pl.ds(pl.multiple_of(b * TOK, TOK), TOK)
        kb = kt[r]
        hb = ht[r]
        for t, g in enumerate((mm(kb, dg[...]), mm(kb, du[...]), -mm(hb, vh[...]))):
            own[b, t] = jnp.where(first, g[:, :HALF], g[:, HALF:])
            gsend[b, t] = jnp.where(first, g[:, HALF:], g[:, :HALF]).astype(BF16)
        g_copy(b).start()

    loop(NX, grad)

    def pair(i):
        b = lax.rem(x + 1 + i, NX)
        g_copy(b).wait_recv()
        for t in range(3):
            for j in range(4):
                total = own[b, t, j * 32 : (j + 1) * 32] + grecv[b, t, j * 32 : (j + 1) * 32].astype(F32)
                xs[b, j, t] = total.astype(BF16)

    loop(NX, pair)

    def part_of(j):
        return lax.rem(lax.div(z, 4) + 2 + j, 4)

    def rx_copy(j, e):
        to = lax.rem(x + e, NX)
        p = part_of(j)
        return remote(xs.at[to, p], xr.at[e, p], rx_s.at[e, p], rx_r.at[e, p], wide_0=to)

    def rx_start(j):
        for e in (1, 3, 2):
            rx_copy(j, e).start()

    loop(4, rx_start)

    tok_wait(2)
    gains = gain[:, cols(y)]
    e0 = lengths[0, 0]
    e1 = e0 + lengths[0, 1]
    e2 = e1 + lengths[0, 2]

    def ids(pos):
        return (
            (pos >= e0).astype(jnp.int32) + (pos >= e1).astype(jnp.int32) + (pos >= e2).astype(jnp.int32)
        )

    def attend(i):
        r = pl.ds(pl.multiple_of(i * TOK, TOK), TOK)
        scores = nt(qh[r], kh[...]) * (HEAD**-0.5)
        qid = ids(lax.broadcasted_iota(jnp.int32, (TOK, GROUP), 0) + i * TOK)
        kid = ids(lax.broadcasted_iota(jnp.int32, (TOK, GROUP), 1))
        scores = jnp.where(qid == kid, scores, -1e30)
        expo = jnp.exp(scores - jnp.max(scores, axis=-1, keepdims=True))
        probs = (expo / jnp.sum(expo, axis=-1, keepdims=True)).astype(BF16)
        view[r] = rms(mm(probs, vh[...]), gains).astype(BF16)

    loop(4, attend)

    def rz_copy(to):
        return remote(zs.at[to], zr.at[z], rz_s.at[to], rz_r.at[z], wide_1=to)

    def fold(j):
        p = part_of(j)
        for e in range(1, NX):
            remote(xs.at[x, p], xr.at[e, p], rx_s.at[e, p], rx_r.at[e, p], wide_0=x).wait_recv()
        total = xs[x, p].astype(F32)
        for e in range(1, NX):
            total = total + xr[e, p].astype(F32)
        for t in range(4):
            zs[p * 4 + t] = total[:, t * 8 : (t + 1) * 8].astype(BF16)
        for t in range(4):

            @pl.when(p * 4 + t != z)
            def _():
                rz_copy(p * 4 + t).start()

    loop(4, fold)
    zr[z] = zs[z]
    gather_sent(wbuf, wz_s, wz_r, wx_s, wx_r, wc_s, wc_r)

    def summed(d, total):
        frm = lax.rem(z + NZ - d, NZ)
        remote(zs.at[frm], zr.at[frm], rz_s.at[frm], rz_r.at[frm], wide_1=frm).wait_recv()
        return total + zr[frm].astype(F32)

    total = lax.fori_loop(1, NZ, summed, zr[z].astype(F32))
    mbuf[chip, c] = (momentum_decay * mhalf[...] + total * TOKENS**-0.5).astype(BF16)
    gather(mbuf, mz_s, mz_r, mx_s, mx_r, mc_s, mc_r)

    def squares(i, sums):
        b = pl.ds(pl.multiple_of(i * NZ, NZ), NZ)
        return tuple(
            s + jnp.sum(jnp.square(mbuf[b, 0, t].astype(F32)) + jnp.square(mbuf[b, 1, t].astype(F32)), axis=0)
            for t, s in enumerate(sums)
        )

    blank = jnp.zeros((8, HALF), F32)
    sums = lax.fori_loop(0, NX, squares, (blank, blank, blank))
    steps = tuple(
        step_size * lax.rsqrt(jnp.sum(jnp.sum(s, axis=1, keepdims=True), axis=0, keepdims=True) / HEAD**2 + epsilon)
        for s in sums
    )

    def moved_rows(w0, w1, m0, m1, step):
        v0 = w0 - m0 * step
        v1 = w1 - m1 * step
        before = jnp.sum(w0 * w0 + w1 * w1, axis=-1, keepdims=True) + epsilon
        after = jnp.sum(v0 * v0 + v1 * v1, axis=-1, keepdims=True) + epsilon
        ratio = jnp.sqrt(before) / jnp.sqrt(after)
        return v0 * ratio, v1 * ratio

    def renew(i):
        r = pl.ds(pl.multiple_of(i * TOK, TOK), TOK)
        b = pl.ds(pl.multiple_of(i * NZ, NZ), NZ)
        for t in range(3):
            parts = moved_rows(
                *(
                    buf[b, h, t].astype(F32).reshape(TOK, HALF)
                    for buf in (wbuf, mbuf)
                    for h in range(2)
                ),
                steps[t],
            )
            for h in range(2):
                n2[t, r, h * HALF : (h + 1) * HALF] = parts[h].astype(BF16)

    loop(4, renew)
    for d in range(1, NY):
        tok_copy(2, d).wait_send()

    def o_copy(i):
        to = lax.rem(y + 1 + i, NY)
        return remote(oblk.at[i], out.at[:, cols(y)], o_s.at[i], o_r.at[i], narrow=to)

    def apply(i):
        r = rows(lax.rem(y + 1 + i, NY))
        qb = qh[r]
        pre_gate = mm(qb, n2[0])
        pre_up = mm(qb, n2[1])
        hidden = (pre_gate * jax.nn.sigmoid(pre_gate) * pre_up).astype(BF16)
        fast = rms(mm(hidden, n2[2]), gains).astype(BF16)
        oblk[i] = (view[r].astype(F32) + fast.astype(F32)).astype(BF16)

        @pl.when(i < NY - 1)
        def _():
            o_copy(i).start()

    loop(NY, apply)
    keep = pltpu.make_async_copy(oblk.at[NY - 1], out.at[:, cols(y)], o_own)
    keep.start()

    for t, (new, mom) in enumerate(((ng, og), (nu, ou), (nd, od))):
        m0, m1 = mbuf[chip, 0, t].astype(F32), mbuf[chip, 1, t].astype(F32)
        parts = moved_rows(wbuf[chip, 0, t].astype(F32), wbuf[chip, 1, t].astype(F32), m0, m1, steps[t])
        whole = jnp.concatenate(parts, axis=1)
        new[0] = jnp.where(first, whole[:4], whole[4:]).astype(BF16)
        whole = jnp.concatenate([m0, m1], axis=1)
        mom[0] = jnp.where(first, whole[:4], whole[4:])

    swap.wait_send()
    for t in range(2):
        for d in range(1, NY):
            tok_copy(t, d).wait_send()
    for b in range(NX):
        g_copy(b).wait_send()
    for j in range(4):
        for e in range(1, NX):
            rx_copy(j, e).wait_send()

    def z_sent(d):
        rz_copy(lax.rem(z + d, NZ)).wait_send()

    loop(NZ, z_sent, 1)
    gather_sent(mbuf, mz_s, mz_r, mx_s, mx_r, mc_s, mc_r)
    for i in range(NY - 1):
        frm = lax.rem(y + NY - 1 - i, NY)
        remote(oblk.at[i], out.at[:, cols(frm)], o_s.at[i], o_r.at[i], narrow=frm).wait()
    keep.wait()


def per_device(queries, keys, values, view_lengths, gain, *weights):
    vmem = pl.BlockSpec(memory_space=pltpu.VMEM)
    anywhere = pl.BlockSpec(memory_space=pl.ANY)
    dma = pltpu.SemaphoreType.DMA
    sq = (HEAD, HEAD)
    gather_sems = [dma((NZ,)), dma((NZ,)), dma((NX, NZ)), dma((NX, NZ)), dma((NX,)), dma((NX,))]
    return pl.pallas_call(
        kernel,
        out_shape=(
            jax.ShapeDtypeStruct(queries.shape, BF16),
            *(jax.ShapeDtypeStruct((1, 4, HEAD), BF16) for _ in range(3)),
            *(jax.ShapeDtypeStruct((1, 4, HEAD), F32) for _ in range(3)),
        ),
        in_specs=[anywhere] * 3 + [pl.BlockSpec(memory_space=pltpu.SMEM)] + [vmem] * 7,
        out_specs=(anywhere, *[vmem] * 6),
        scratch_shapes=[
            *[pltpu.VMEM(sq, BF16)] * 8,
            pltpu.VMEM((6, 4, HEAD), F32),
            pltpu.VMEM((6, 4, HEAD), F32),
            pltpu.VMEM((3, 8, HALF), F32),
            pltpu.VMEM((CHIPS, 2, 3, 8, HALF), BF16),
            pltpu.VMEM((3, HEAD, HEAD), BF16),
            pltpu.VMEM((NX, 3, TOK, HALF), F32),
            pltpu.VMEM((NX, 3, TOK, HALF), BF16),
            pltpu.VMEM((NX, 3, TOK, HALF), BF16),
            pltpu.VMEM((NX, 4, 3, 32, HALF), BF16),
            pltpu.VMEM((NX, 4, 3, 32, HALF), BF16),
            pltpu.VMEM((NZ, 3, 8, HALF), BF16),
            pltpu.VMEM((NZ, 3, 8, HALF), BF16),
            pltpu.VMEM((CHIPS, 2, 3, 8, HALF), BF16),
            pltpu.VMEM((3, HEAD, HEAD), BF16),
            pltpu.VMEM(sq, BF16),
            pltpu.VMEM((NY, TOK, HEAD), BF16),
            dma((3, NY)), dma((3, NY)), dma((3,)), dma((2,)),
            *gather_sems,
            *gather_sems,
            dma((NX,)), dma((NX,)), dma((NX, 4)), dma((NX, 4)), dma((NZ,)), dma((NZ,)),
            dma((NY,)), dma((NY,)), dma,
        ],
        compiler_params=pltpu.CompilerParams(
            collective_id=0, has_side_effects=True, vmem_limit_bytes=48 * 1024 * 1024
        ),
    )(queries, keys, values, view_lengths, gain.reshape(1, -1), *weights)


def solution(mesh):
    split = Mesh(
        mesh.devices.reshape(NX, NZ, 2, mesh.shape["narrow"]),
        ("wide_0", "wide_1", "wide_2", "narrow"),
    )
    rows = P("narrow", WIDE, None)
    return jax.shard_map(
        per_device,
        mesh=split,
        in_specs=(*[P(WIDE_NARROW, None)] * 3, P(WIDE, None), P(), *[rows] * 6),
        out_specs=(P(WIDE_NARROW, None), *[rows] * 6),
        check_vma=False,
    )
```

time: 361 us -> 106 us (0.29)
  waiting for transfers between devices: 141 us -> 0 us
  Pallas kernels: 0 us -> 92.1 us
  starting transfers between devices: 83.6 us -> 0 us
  blocking collectives: 45.5 us -> 0 us
  local copies, waits for them, and re-layouts: 47.5 us -> 13 us
  other arithmetic: 23.3 us -> 0 us
  matrix products: 13.9 us -> 0 us
    all_to_all x12 -> x0, waiting for transfers between devices: 141 us -> none  [the longest x4 72.4 us: copy_for_each(): lax.all_to_all(jnp.broadcast_to(array[None], (size, *array.shape)), axis,...]
    pallas_call x0 -> x1, Pallas kernels: none -> 92.1 us  [per_device(): pl.pallas_call(kernel, out_shape=(jax.ShapeDtypeStruct(queries.shape, BF1...]
    all_to_all x12 -> x0, starting transfers between devices: 83.6 us -> none  [the longest x4 40.3 us: copy_for_each(): lax.all_to_all(jnp.broadcast_to(array[None], (size, *array.shape)), axis,...]
    all_to_all x7 -> x0, blocking collectives: 45.5 us -> none  [the longest x4 30 us: copy_for_each(): lax.all_to_all(jnp.broadcast_to(array[None], (size, *array.shape)), axis,...]
    dot_general x10 -> x0, matrix products: 13.9 us -> none  [the longest x1 2.47 us: one_block(): fast_raw = jnp.dot(hidden, down_full, preferred_element_type=jnp.float32)]
    convert_element_type x9 -> x0, local copies, waits for them, and re-layouts: 12.3 us -> none  [the longest x6 10.2 us: total_of(): lax.slice_in_dim(whole, 0, len(lines)).reshape(array.shape)]
    reduce_sum x12 -> x0, other arithmetic: 12.3 us -> none  [the longest x3 4.58 us: sent_and_summed(): return jnp.sum(parts.astype(jnp.float32), axis=0)]
    broadcast_in_dim x14 -> x0, local copies, waits for them, and re-layouts: 10.7 us -> none  [the longest x8 4.25 us: copy_for_each(): jnp.broadcast_to(array[None], (size, *array.shape))]
  transfers between devices with their start and end apart: 12 -> 0, of which waited for: 10 -> 0; matrix products, arithmetic and copies ran while one was open for 17% -> 0% of each run, Pallas kernels for 0% -> 0%
where the time goes in v1:
time: 106 us
  Pallas kernels  92.1 us (87%)
  local copies, waits for them, and re-layouts  13 us (12%)
    pallas_call x1, Pallas kernels, per_device(): pl.pallas_call(kernel, out_shape=(jax.ShapeDtypeStruct(queries.shape, BF1...  92.1 us
    unnamed x29, local copies, waits for them, and re-layouts  13 us

profile of v1, /device:TPU:1, one launch (start us, length us, event | category | flops | bytes accessed | tf_op | source)
XLA Modules:
  0.0 105.7 jit_solution(2192336159277661558)
XLA Ops:
  0.6 0.0 copy-start.10
  0.6 0.6 copy-done.10
  1.3 0.0 copy-start
  1.3 1.0 copy-done
  2.3 0.0 copy-start.1
  2.3 1.0 copy-done.1
  3.4 0.0 copy-start.2
  3.4 1.0 copy-done.2
  4.4 0.0 copy-start.3
  4.4 0.7 copy-done.3
  5.1 0.7 copy-done.4
  5.8 0.7 copy-done.5
  6.5 0.7 copy-done.6
  7.2 0.7 copy-done.7
  7.9 0.7 copy-done.8
  8.6 0.7 copy-done.9
  9.3 92.1 %shard_map.162 = (bf16[128,2048]{1,0:T(8,128)(2,1)S(1)}, bf16[1,4,512]{2,1,0:T(4,128)(2,1)S(1)}, bf16[1,4,512]{2,1,0:T(4,128)(2,1)S(1)}, bf16[1,4,512]{2,1,0:T(4...) custom-call(bf16[128,2048]{1,0:T(8,128)(2,1)S(1)} %copy-done, ...), custom_call_target="tpu_custom_call" | custom-call | tf_op jit(solution)/shard_map/pallas_call | solution.py:432
  101.4 0.8 copy.25
  102.2 0.6 copy.26
  102.8 0.6 copy.27
  103.4 0.6 copy.28
  104.0 0.6 copy.29
  104.6 0.6 copy.30
  105.2 0.6 copy.31
  (6 shorter events, 0.0 us)
Async XLA Ops:
  0.6 0.7 copy-start.10
  1.3 1.0 copy-start
  2.3 1.0 copy-start.1
  3.4 1.0 copy-start.2
  4.4 0.7 copy-start.3
  5.1 0.7 copy-start.4
  5.8 0.7 copy-start.5
  6.5 0.7 copy-start.6
  7.2 0.7 copy-start.7
  7.9 0.7 copy-start.8
  8.6 0.7 copy-start.9

commit v2 on v1

--- a/solution.py
+++ b/solution.py
@@ -17,6 +17,7 @@
 epsilon = 1e-06
 
 NX, NZ, NY = 4, 16, 4
+NEAR = 4
 HEAD = 512
 HALF = 256
 GROUP = 512
@@ -54,8 +55,9 @@
 
 
 def kernel(
-    q_in, k_in, v_in, lengths, gain, wg, wu, wd, mg, mu, md,
-    out, ng, nu, nd, og, ou, od,
+    q_in, k_in, v_in, lengths_in, gain_in, wg, wu, wd, mg, mu, md,
+    out, new_out, mom_out,
+    lengths, gain, wrow, newv, momv, small_sem,
     qh, kh, vh, kt, ht, hid, dg, du, ex, exr, mhalf, wbuf, w2, own, gsend, grecv,
     xs, xr, zs, zr, mbuf, n2, view, oblk,
     tok_send, tok_recv, tok_own, ex_sem, wz_s, wz_r, wx_s, wx_r, wc_s, wc_r,
@@ -68,10 +70,14 @@
     chip = x * NZ + z
     other = 1 - c
 
-    for t, w in enumerate((wg, wu, wd)):
-        ex[t] = w[0].astype(F32)
-    for t, m in enumerate((mg, mu, md)):
-        ex[3 + t] = m[0]
+    small = [pltpu.make_async_copy(w.at[0], wrow.at[t], small_sem.at[t]) for t, w in enumerate((wg, wu, wd))]
+    small += [pltpu.make_async_copy(m.at[0], ex.at[3 + t], small_sem.at[3 + t]) for t, m in enumerate((mg, mu, md))]
+    small += [
+        pltpu.make_async_copy(lengths_in, lengths, small_sem.at[6]),
+        pltpu.make_async_copy(gain_in, gain, small_sem.at[7]),
+    ]
+    for copy in small:
+        copy.start()
 
     barrier = pltpu.get_barrier_semaphore()
     pl.semaphore_signal(barrier, inc=1, device_id={"wide_2": other}, device_id_type=MESH)
@@ -89,8 +95,13 @@
             barrier, inc=1, device_id={"wide_1": lax.rem(z + d, NZ)}, device_id_type=MESH
         )
 
-    loop(NZ, greet, 1)
-    pl.semaphore_wait(barrier, NY - 1 + NX - 1 + NZ - 1 + 1)
+    for d in range(1, NEAR + 1):
+        greet(d)
+        greet(NZ - d)
+    for copy in small:
+        copy.wait()
+    ex[:3] = wrow[...].astype(F32)
+    pl.semaphore_wait(barrier, NY - 1 + NX - 1 + 2 * NEAR + 1)
 
     def cols(who):
         return pl.ds(pl.multiple_of(who * HEAD, HEAD), HEAD)
@@ -141,49 +152,64 @@
             buf.at[b, c], buf.at[b, c], s.at[e, d], r.at[e, d], wide_0=lax.rem(x + e, NX)
         )
 
-    def c_copy(buf, s, r, e):
-        first = pl.multiple_of(lax.rem(x + NX - e, NX) * NZ, NZ)
-        part = buf.at[pl.ds(first, NZ), c]
-        return remote(part, part, s.at[e], r.at[e], wide_2=other)
+    def z_relay(buf, s, r, via, d):
+        hop = d - via if d <= NZ // 2 else NZ - (via - d)
+        b = block_of(via)
+        return remote(
+            buf.at[b, c], buf.at[b, c], s.at[d], r.at[d], wide_1=lax.rem(z + hop, NZ)
+        )
 
     def gather(buf, z_s, z_r, x_s, x_r, c_s, c_r):
-        for d in range(1, NZ // 2):
-            z_copy(buf, z_s, z_r, d).start()
-            z_copy(buf, z_s, z_r, NZ - d).start()
-        z_copy(buf, z_s, z_r, NZ // 2).start()
-
         def forward(d):
             for e in (1, 3, 2):
                 x_copy(buf, x_s, x_r, e, d).start()
 
-        forward(0)
-
-        def relay(d):
+        def landed(d):
             b = block_of(d)
             remote(buf.at[b, c], buf.at[b, c], z_s.at[d], z_r.at[d], wide_1=z).wait_recv()
-            forward(d)
-
-        def relay_pair(d):
-            relay(d)
-            relay(NZ - d)
-
-        loop(NZ // 2, relay_pair, 1)
-        relay(NZ // 2)
-        c_copy(buf, c_s, c_r, 0).start()
-        for e in (1, 3, 2):
-
-            def landed(d, e=e):
+
+        def across(b):
+            remote(buf.at[b, c], buf.at[b, c], c_s, c_r, wide_2=other).start()
+
+        for d in range(NEAR, 0, -1):
+            z_copy(buf, z_s, z_r, d).start()
+            z_copy(buf, z_s, z_r, NZ - d).start()
+        forward(0)
+        across(chip)
+        for d in range(1, NEAR + 1):
+            for o in (d, NZ - d):
+                landed(o)
+                if d == NEAR:
+                    for n in range(NEAR, 0, -1):
+                        if o == NEAR:
+                            z_relay(buf, z_s, z_r, o, NEAR + n).start()
+                        elif NEAR + n < NZ // 2:
+                            z_relay(buf, z_s, z_r, o, NZ - NEAR - n).start()
+                forward(o)
+                across(block_of(o))
+        for d in range(NEAR + 1, NZ // 2 + 1):
+            for o in (d, NZ - d) if d < NZ // 2 else (d,):
+                landed(o)
+                forward(o)
+                across(block_of(o))
+
+        def arrived(d):
+            for e in (1, 3, 2):
                 b = lax.rem(x + NX - e, NX) * NZ + lax.rem(z + NZ - d, NZ)
                 remote(
                     buf.at[b, c], buf.at[b, c], x_s.at[e, d], x_r.at[e, d], wide_0=x
                 ).wait_recv()
-
-            loop(NZ, landed)
-            c_copy(buf, c_s, c_r, e).start()
-        for e in range(NX):
-            first = pl.multiple_of(lax.rem(x + NX - e, NX) * NZ, NZ)
-            part = buf.at[pl.ds(first, NZ), other]
-            remote(part, part, c_s.at[e], c_r.at[e], wide_2=other).wait_recv()
+                across(b)
+
+        arrived(0)
+
+        def arrived_pair(d):
+            arrived(d)
+            arrived(NZ - d)
+
+        loop(NZ // 2, arrived_pair, 1)
+        arrived(NZ // 2)
+        remote(buf.at[:, other], buf.at[:, other], c_s, c_r, wide_2=other).wait_recv()
 
     def gather_sent(buf, z_s, z_r, x_s, x_r, c_s, c_r):
         def far(d):
@@ -196,8 +222,7 @@
                 x_copy(buf, x_s, x_r, e, d).wait_send()
 
         loop(NZ, near)
-        for e in range(NX):
-            c_copy(buf, c_s, c_r, e).wait_send()
+        remote(buf.at[:, c], buf.at[:, c], c_s, c_r, wide_2=other).wait_send()
 
     swap.wait_recv()
     mine, theirs = ex[...], exr[...]
@@ -394,13 +419,19 @@
     keep = pltpu.make_async_copy(oblk.at[NY - 1], out.at[:, cols(y)], o_own)
     keep.start()
 
-    for t, (new, mom) in enumerate(((ng, og), (nu, ou), (nd, od))):
+    for t in range(3):
         m0, m1 = mbuf[chip, 0, t].astype(F32), mbuf[chip, 1, t].astype(F32)
         parts = moved_rows(wbuf[chip, 0, t].astype(F32), wbuf[chip, 1, t].astype(F32), m0, m1, steps[t])
         whole = jnp.concatenate(parts, axis=1)
-        new[0] = jnp.where(first, whole[:4], whole[4:]).astype(BF16)
+        newv[t] = jnp.where(first, whole[:4], whole[4:]).astype(BF16)
         whole = jnp.concatenate([m0, m1], axis=1)
-        mom[0] = jnp.where(first, whole[:4], whole[4:])
+        momv[t] = jnp.where(first, whole[:4], whole[4:])
+    done = [
+        pltpu.make_async_copy(newv, new_out, small_sem.at[0]),
+        pltpu.make_async_copy(momv, mom_out, small_sem.at[1]),
+    ]
+    for copy in done:
+        copy.start()
 
     swap.wait_send()
     for t in range(2):
@@ -421,27 +452,56 @@
         frm = lax.rem(y + NY - 1 - i, NY)
         remote(oblk.at[i], out.at[:, cols(frm)], o_s.at[i], o_r.at[i], narrow=frm).wait()
     keep.wait()
+    for copy in done:
+        copy.wait()
+
+
+def deliver(out_in, new_in, mom_in, out, ng, nu, nd, og, ou, od, outv, newv, momv, sems):
+    quarter = TOK // 4
+    parts = [pl.ds(i * quarter, quarter) for i in range(4)]
+    get = [pltpu.make_async_copy(new_in, newv, sems.at[0]), pltpu.make_async_copy(mom_in, momv, sems.at[1])]
+    get += [pltpu.make_async_copy(out_in.at[p], outv.at[p], sems.at[2 + i]) for i, p in enumerate(parts)]
+    put = [
+        [pltpu.make_async_copy(newv.at[t], o.at[0], sems.at[6 + t]) for t, o in enumerate((ng, nu, nd))],
+        [pltpu.make_async_copy(momv.at[t], o.at[0], sems.at[9 + t]) for t, o in enumerate((og, ou, od))],
+        *([pltpu.make_async_copy(outv.at[p], out.at[p], sems.at[12 + i])] for i, p in enumerate(parts)),
+    ]
+    for copy in get:
+        copy.start()
+    for copy, then in zip(get, put):
+        copy.wait()
+        for other in then:
+            other.start()
+    for then in put:
+        for other in then:
+            other.wait()
 
 
 def per_device(queries, keys, values, view_lengths, gain, *weights):
-    vmem = pl.BlockSpec(memory_space=pltpu.VMEM)
-    anywhere = pl.BlockSpec(memory_space=pl.ANY)
+    hbm = pl.BlockSpec(memory_space=pltpu.HBM)
     dma = pltpu.SemaphoreType.DMA
     sq = (HEAD, HEAD)
-    gather_sems = [dma((NZ,)), dma((NZ,)), dma((NX, NZ)), dma((NX, NZ)), dma((NX,)), dma((NX,))]
-    return pl.pallas_call(
+    row = (4, HEAD)
+    gather_sems = [dma((NZ,)), dma((NZ,)), dma((NX, NZ)), dma((NX, NZ)), dma, dma]
+    parts = pl.pallas_call(
         kernel,
         out_shape=(
             jax.ShapeDtypeStruct(queries.shape, BF16),
-            *(jax.ShapeDtypeStruct((1, 4, HEAD), BF16) for _ in range(3)),
-            *(jax.ShapeDtypeStruct((1, 4, HEAD), F32) for _ in range(3)),
+            jax.ShapeDtypeStruct((3, *row), BF16),
+            jax.ShapeDtypeStruct((3, *row), F32),
         ),
-        in_specs=[anywhere] * 3 + [pl.BlockSpec(memory_space=pltpu.SMEM)] + [vmem] * 7,
-        out_specs=(anywhere, *[vmem] * 6),
+        in_specs=[hbm] * 11,
+        out_specs=(hbm,) * 3,
         scratch_shapes=[
+            pltpu.SMEM(view_lengths.shape, jnp.int32),
+            pltpu.VMEM((1, gain.shape[0]), F32),
+            pltpu.VMEM((3, *row), BF16),
+            pltpu.VMEM((3, *row), BF16),
+            pltpu.VMEM((3, *row), F32),
+            dma((8,)),
             *[pltpu.VMEM(sq, BF16)] * 8,
-            pltpu.VMEM((6, 4, HEAD), F32),
-            pltpu.VMEM((6, 4, HEAD), F32),
+            pltpu.VMEM((6, *row), F32),
+            pltpu.VMEM((6, *row), F32),
             pltpu.VMEM((3, 8, HALF), F32),
             pltpu.VMEM((CHIPS, 2, 3, 8, HALF), BF16),
             pltpu.VMEM((3, HEAD, HEAD), BF16),
@@ -463,9 +523,26 @@
             dma((NY,)), dma((NY,)), dma,
         ],
         compiler_params=pltpu.CompilerParams(
-            collective_id=0, has_side_effects=True, vmem_limit_bytes=48 * 1024 * 1024
+            collective_id=0, has_side_effects=True, vmem_limit_bytes=67_043_328
         ),
     )(queries, keys, values, view_lengths, gain.reshape(1, -1), *weights)
+    return pl.pallas_call(
+        deliver,
+        out_shape=(
+            jax.ShapeDtypeStruct(queries.shape, BF16),
+            *[jax.ShapeDtypeStruct((1, *row), BF16)] * 3,
+            *[jax.ShapeDtypeStruct((1, *row), F32)] * 3,
+        ),
+        in_specs=[hbm] * 3,
+        out_specs=(hbm,) * 7,
+        scratch_shapes=[
+            pltpu.VMEM(queries.shape, BF16),
+            pltpu.VMEM((3, *row), BF16),
+            pltpu.VMEM((3, *row), F32),
+            dma((16,)),
+        ],
+        compiler_params=pltpu.CompilerParams(vmem_limit_bytes=67_043_328),
+    )(*parts)
 
 
 def solution(mesh):

time: 106 us -> 91.3 us (0.86)
  local copies, waits for them, and re-layouts: 13 us -> 0 us
  Pallas kernels: 92.1 us -> 90.3 us
    unnamed x29 -> x0, local copies, waits for them, and re-layouts: 13 us -> none
    pallas_call x1, Pallas kernels: 92.1 us -> 88.4 us  [per_device(): pl.pallas_call(kernel, out_shape=(jax.ShapeDtypeStruct(queries.shape, BF1...]
    pallas_call x0 -> x1, Pallas kernels: none -> 1.93 us  [per_device(): pl.pallas_call(deliver, out_shape=(jax.ShapeDtypeStruct(queries.shape, BF...]
where the time goes in v2:
time: 91.3 us; the launch traced here: 91 us
  Pallas kernels  90.3 us (99%)
    pallas_call x1, Pallas kernels, per_device(): pl.pallas_call(kernel, out_shape=(jax.ShapeDtypeStruct(queries.shape, BF1...  88.4 us
    pallas_call x1, Pallas kernels, per_device(): pl.pallas_call(deliver, out_shape=(jax.ShapeDtypeStruct(queries.shape, BF...  1.93 us

profile of v2, /device:TPU:1, one launch (start us, length us, event | category | flops | bytes accessed | tf_op | source)
XLA Modules:
  0.0 91.0 jit_solution(15310135352166295772)
XLA Ops:
  0.6 88.4 %shard_map.162 = (bf16[128,2048]{1,0:T(8,128)(2,1)}, bf16[3,4,512]{2,1,0:T(4,128)(2,1)}, f32[3,4,512]{2,1,0:T(4,128)}) custom-call(bf16[128,2048]{1,0:T(8,128)(2,1)} %q_in.1, bf16[128,2048]{1,0:T(8,128)(2,1)} %k_in.1, bf16[128,2048]{1,0:T(8,128)(2,1)} %v_in.1, s32[1,4]{1,0:T(1,128)} %lengths_in.1, f32[1,2048]{1,0:T(1,128)} %bitcast.1, ...), custom_call_target="tpu_custom_call" | custom-call | tf_op jit(solution)/shard_map/pallas_call | solution.py:486
  89.1 1.9 %shard_map.163 = (bf16[128,2048]{1,0:T(8,128)(2,1)}, bf16[1,4,512]{2,1,0:T(4,128)(2,1)}, bf16[1,4,512]{2,1,0:T(4,128)(2,1)}, bf16[1,4,512]{2,1,0:T(4,128)(2,1)},...) custom-call(bf16[128,2048]{1,0:T(8,128)(2,1)} %get-tuple-element.10.out_in, ...), custom_call_target="tpu_custom_call" | custom-call | tf_op jit(solution)/shard_map/pallas_call | solution.py:529

commit v3 on v2

--- a/solution.py
+++ b/solution.py
@@ -159,9 +159,9 @@
             buf.at[b, c], buf.at[b, c], s.at[d], r.at[d], wide_1=lax.rem(z + hop, NZ)
         )
 
-    def gather(buf, z_s, z_r, x_s, x_r, c_s, c_r):
-        def forward(d):
-            for e in (1, 3, 2):
+    def gather(buf, z_s, z_r, x_s, x_r, c_s, c_r, meanwhile=None):
+        def forward(d, order=(1, 3, 2)):
+            for e in order:
                 x_copy(buf, x_s, x_r, e, d).start()
 
         def landed(d):
@@ -170,6 +170,17 @@
 
         def across(b):
             remote(buf.at[b, c], buf.at[b, c], c_s, c_r, wide_2=other).start()
+
+        def arrived(d, onward=()):
+            for e in (1, 3, 2):
+                b = lax.rem(x + NX - e, NX) * NZ + lax.rem(z + NZ - d, NZ)
+                remote(
+                    buf.at[b, c], buf.at[b, c], x_s.at[e, d], x_r.at[e, d], wide_0=x
+                ).wait_recv()
+                for n in onward:
+                    to = lax.rem(z + NZ + n - d, NZ)
+                    remote(buf.at[b, c], buf.at[b, c], x_s.at[e, n], x_r.at[e, n], wide_1=to).start()
+                across(b)
 
         for d in range(NEAR, 0, -1):
             z_copy(buf, z_s, z_r, d).start()
@@ -187,27 +198,25 @@
                             z_relay(buf, z_s, z_r, o, NZ - NEAR - n).start()
                 forward(o)
                 across(block_of(o))
-        for d in range(NEAR + 1, NZ // 2 + 1):
-            for o in (d, NZ - d) if d < NZ // 2 else (d,):
-                landed(o)
-                forward(o)
-                across(block_of(o))
-
-        def arrived(d):
-            for e in (1, 3, 2):
-                b = lax.rem(x + NX - e, NX) * NZ + lax.rem(z + NZ - d, NZ)
-                remote(
-                    buf.at[b, c], buf.at[b, c], x_s.at[e, d], x_r.at[e, d], wide_0=x
-                ).wait_recv()
-                across(b)
-
         arrived(0)
+        arrived(4, (6, 5))
+        arrived(12, (10, 11))
+        for o in (7, 9, 8):
+            landed(o)
+            forward(o, (2, 1, 3))
+            across(block_of(o))
+        for o in (5, 11, 6, 10):
+            landed(o)
+            across(block_of(o))
+        if meanwhile is not None:
+            meanwhile()
 
         def arrived_pair(d):
             arrived(d)
             arrived(NZ - d)
 
-        loop(NZ // 2, arrived_pair, 1)
+        loop(NEAR, arrived_pair, 1)
+        loop(NZ // 2, arrived_pair, NEAR + 1)
         arrived(NZ // 2)
         remote(buf.at[:, other], buf.at[:, other], c_s, c_r, wide_2=other).wait_recv()
 
@@ -233,7 +242,12 @@
     half = jnp.where(first, rows8[:, :, :HALF], rows8[:, :, HALF:])
     wbuf[chip, c] = half[:3].astype(BF16)
     mhalf[...] = half[3:]
-    gather(wbuf, wz_s, wz_r, wx_s, wx_r, wc_s, wc_r)
+
+    def turn_keys():
+        tok_wait(0)
+        kt[...] = kh[...].T
+
+    gather(wbuf, wz_s, wz_r, wx_s, wx_r, wc_s, wc_r, turn_keys)
 
     def square(i):
         r = pl.ds(pl.multiple_of(i * TOK, TOK), TOK)
@@ -244,10 +258,8 @@
                 w2[t, r, h * HALF : (h + 1) * HALF] = part.astype(BF16)
 
     loop(4, square)
-    tok_wait(0)
     tok_wait(1)
 
-    kt[...] = kh[...].T
 
     def back(i):
         r = pl.ds(pl.multiple_of(i * TOK, TOK), TOK)
@@ -267,41 +279,43 @@
     def g_copy(b):
         return remote(gsend.at[b], grecv.at[b], gs_s.at[b], gs_r.at[b], wide_2=other)
 
-    def grad(i):
-        b = lax.rem(x + 1 + i, NX)
-        r = pl.ds(pl.multiple_of(b * TOK, TOK), TOK)
-        kb = kt[r]
-        hb = ht[r]
+    def part_of(j):
+        return lax.rem(lax.div(z, 4) + 2 + j + lax.div(j * (j - 1), 2), 4)
+
+    def grad(j):
+        p = part_of(j)
+        quarter = [pl.ds(pl.multiple_of(b * TOK + p * 32, 32), 32) for b in range(NX)]
+        kb = jnp.concatenate([kt[r] for r in quarter], axis=0)
+        hb = jnp.concatenate([ht[r] for r in quarter], axis=0)
         for t, g in enumerate((mm(kb, dg[...]), mm(kb, du[...]), -mm(hb, vh[...]))):
-            own[b, t] = jnp.where(first, g[:, :HALF], g[:, HALF:])
-            gsend[b, t] = jnp.where(first, g[:, HALF:], g[:, :HALF]).astype(BF16)
-        g_copy(b).start()
-
-    loop(NX, grad)
-
-    def pair(i):
-        b = lax.rem(x + 1 + i, NX)
-        g_copy(b).wait_recv()
-        for t in range(3):
-            for j in range(4):
-                total = own[b, t, j * 32 : (j + 1) * 32] + grecv[b, t, j * 32 : (j + 1) * 32].astype(F32)
-                xs[b, j, t] = total.astype(BF16)
-
-    loop(NX, pair)
-
-    def part_of(j):
-        return lax.rem(lax.div(z, 4) + 2 + j, 4)
+            keep = jnp.where(first, g[:, :HALF], g[:, HALF:])
+            give = jnp.where(first, g[:, HALF:], g[:, :HALF]).astype(BF16)
+            for b in range(NX):
+                own[p, b, t] = keep[b * 32 : (b + 1) * 32]
+                gsend[p, b, t] = give[b * 32 : (b + 1) * 32]
+        g_copy(p).start()
 
     def rx_copy(j, e):
         to = lax.rem(x + e, NX)
         p = part_of(j)
         return remote(xs.at[to, p], xr.at[e, p], rx_s.at[e, p], rx_r.at[e, p], wide_0=to)
 
-    def rx_start(j):
+    def pair(j):
+        p = part_of(j)
+        g_copy(p).wait_recv()
+        for b in range(NX):
+            for t in range(3):
+                xs[b, p, t] = (own[p, b, t] + grecv[p, b, t].astype(F32)).astype(BF16)
         for e in (1, 3, 2):
             rx_copy(j, e).start()
 
-    loop(4, rx_start)
+    def grad_and_pair(j):
+        grad(j)
+        pair(j - 1)
+
+    grad(jnp.int32(0))
+    loop(4, grad_and_pair, 1)
+    pair(jnp.int32(3))
 
     tok_wait(2)
     gains = gain[:, cols(y)]
@@ -398,12 +412,15 @@
     for d in range(1, NY):
         tok_copy(2, d).wait_send()
 
+    def turn(i):
+        return 1 + 2 * i - 3 * lax.div(i, 2)
+
     def o_copy(i):
-        to = lax.rem(y + 1 + i, NY)
+        to = lax.rem(y + turn(i), NY)
         return remote(oblk.at[i], out.at[:, cols(y)], o_s.at[i], o_r.at[i], narrow=to)
 
     def apply(i):
-        r = rows(lax.rem(y + 1 + i, NY))
+        r = rows(lax.rem(y + turn(i), NY))
         qb = qh[r]
         pre_gate = mm(qb, n2[0])
         pre_up = mm(qb, n2[1])
@@ -441,15 +458,15 @@
         g_copy(b).wait_send()
     for j in range(4):
         for e in range(1, NX):
-            rx_copy(j, e).wait_send()
+            rx_copy(jnp.int32(j), e).wait_send()
 
     def z_sent(d):
         rz_copy(lax.rem(z + d, NZ)).wait_send()
 
     loop(NZ, z_sent, 1)
     gather_sent(mbuf, mz_s, mz_r, mx_s, mx_r, mc_s, mc_r)
-    for i in range(NY - 1):
-        frm = lax.rem(y + NY - 1 - i, NY)
+    for i, d in enumerate((1, 3, 2)):
+        frm = lax.rem(y + NY - d, NY)
         remote(oblk.at[i], out.at[:, cols(frm)], o_s.at[i], o_r.at[i], narrow=frm).wait()
     keep.wait()
     for copy in done:
@@ -505,9 +522,9 @@
             pltpu.VMEM((3, 8, HALF), F32),
             pltpu.VMEM((CHIPS, 2, 3, 8, HALF), BF16),
             pltpu.VMEM((3, HEAD, HEAD), BF16),
-            pltpu.VMEM((NX, 3, TOK, HALF), F32),
-            pltpu.VMEM((NX, 3, TOK, HALF), BF16),
-            pltpu.VMEM((NX, 3, TOK, HALF), BF16),
+            pltpu.VMEM((4, NX, 3, 32, HALF), F32),
+            pltpu.VMEM((4, NX, 3, 32, HALF), BF16),
+            pltpu.VMEM((4, NX, 3, 32, HALF), BF16),
             pltpu.VMEM((NX, 4, 3, 32, HALF), BF16),
             pltpu.VMEM((NX, 4, 3, 32, HALF), BF16),
             pltpu.VMEM((NZ, 3, 8, HALF), BF16),

time: 91.3 us -> 88.1 us (0.965)
  Pallas kernels: 90.3 us -> 87.2 us
    pallas_call x1, Pallas kernels: 88.4 us -> 85.3 us  [per_device(): pl.pallas_call(kernel, out_shape=(jax.ShapeDtypeStruct(queries.shape, BF1...]
where the time goes in v3:
time: 88.1 us; the launch traced here: 87.8 us
  Pallas kernels  87.2 us (99%)
    pallas_call x1, Pallas kernels, per_device(): pl.pallas_call(kernel, out_shape=(jax.ShapeDtypeStruct(queries.shape, BF1...  85.3 us
    pallas_call x1, Pallas kernels, per_device(): pl.pallas_call(deliver, out_shape=(jax.ShapeDtypeStruct(queries.shape, BF...  1.93 us

profile of v3, /device:TPU:1, one launch (start us, length us, event | category | flops | bytes accessed | tf_op | source)
XLA Modules:
  0.0 87.8 jit_solution(1856282583252260926)
XLA Ops:
  0.6 85.3 %shard_map.162 = (bf16[128,2048]{1,0:T(8,128)(2,1)}, bf16[3,4,512]{2,1,0:T(4,128)(2,1)}, f32[3,4,512]{2,1,0:T(4,128)}) custom-call(bf16[128,2048]{1,0:T(8,128)(2,1)} %q_in.1, bf16[128,2048]{1,0:T(8,128)(2,1)} %k_in.1, bf16[128,2048]{1,0:T(8,128)(2,1)} %v_in.1, s32[1,4]{1,0:T(1,128)} %lengths_in.1, f32[1,2048]{1,0:T(1,128)} %bitcast.1, ...), custom_call_target="tpu_custom_call" | custom-call | tf_op jit(solution)/shard_map/pallas_call | solution.py:503
  85.9 1.9 %shard_map.163 = (bf16[128,2048]{1,0:T(8,128)(2,1)}, bf16[1,4,512]{2,1,0:T(4,128)(2,1)}, bf16[1,4,512]{2,1,0:T(4,128)(2,1)}, bf16[1,4,512]{2,1,0:T(4,128)(2,1)},...) custom-call(bf16[128,2048]{1,0:T(8,128)(2,1)} %get-tuple-element.10.out_in, ...), custom_call_target="tpu_custom_call" | custom-call | tf_op jit(solution)/shard_map/pallas_call | solution.py:546

commit v4 on v3

--- a/solution.py
+++ b/solution.py
@@ -18,11 +18,15 @@
 
 NX, NZ, NY = 4, 16, 4
 NEAR = 4
+RELAY_HOPS = (1, 2, 3, 4)
+OWN_RUN = (0, 1)
+NEAR_RUNS = ((1, 4), (12, 4))
+FAR_RUNS = ((5, 2), (10, 2), (7, 3))
+RUNS = (OWN_RUN, *NEAR_RUNS, *FAR_RUNS)
 HEAD = 512
 HALF = 256
 GROUP = 512
 TOK = 128
-CHIPS = NX * NZ
 TOKENS = 65536
 F32 = jnp.float32
 BF16 = jnp.bfloat16
@@ -67,8 +71,8 @@
     z = lax.axis_index("wide_1")
     c = lax.axis_index("wide_2")
     y = lax.axis_index("narrow")
-    chip = x * NZ + z
     other = 1 - c
+    side = 1 + 2 * c
 
     small = [pltpu.make_async_copy(w.at[0], wrow.at[t], small_sem.at[t]) for t, w in enumerate((wg, wu, wd))]
     small += [pltpu.make_async_copy(m.at[0], ex.at[3 + t], small_sem.at[3 + t]) for t, m in enumerate((mg, mu, md))]
@@ -134,104 +138,83 @@
     swap = remote(ex, exr, ex_sem.at[0], ex_sem.at[1], wide_2=other)
     swap.start()
     for t in range(3):
-        for d in (1, 3, 2):
+        for d in (side, 4 - side, 2):
             tok_copy(t, d).start()
         tok_local(t).start()
 
-    def z_copy(buf, s, r, d):
+    def z_copy(buf, z_s, z_r, via, hop):
+        d = (via + hop) % NZ
         return remote(
-            buf.at[chip, c], buf.at[chip, c], s.at[d], r.at[d], wide_1=lax.rem(z + d, NZ)
-        )
-
-    def block_of(d):
-        return x * NZ + lax.rem(z + NZ - d, NZ)
-
-    def x_copy(buf, s, r, e, d):
-        b = block_of(d)
+            buf.at[0, c, via], buf.at[0, c, d], z_s.at[d], z_r.at[d], wide_1=lax.rem(z + hop, NZ)
+        )
+
+    def x_copy(buf, x_s, x_r, e, k):
+        a, n = RUNS[k]
         return remote(
-            buf.at[b, c], buf.at[b, c], s.at[e, d], r.at[e, d], wide_0=lax.rem(x + e, NX)
-        )
-
-    def z_relay(buf, s, r, via, d):
-        hop = d - via if d <= NZ // 2 else NZ - (via - d)
-        b = block_of(via)
-        return remote(
-            buf.at[b, c], buf.at[b, c], s.at[d], r.at[d], wide_1=lax.rem(z + hop, NZ)
+            buf.at[0, c, pl.ds(a, n)], buf.at[e, c, pl.ds(a, n)], x_s.at[e, k], x_r.at[e, k],
+            wide_0=lax.rem(x + e, NX),
         )
 
     def gather(buf, z_s, z_r, x_s, x_r, c_s, c_r, meanwhile=None):
-        def forward(d, order=(1, 3, 2)):
-            for e in order:
-                x_copy(buf, x_s, x_r, e, d).start()
+        def across(e, k):
+            a, n = RUNS[k]
+            part = buf.at[e, c, pl.ds(a, n)]
+            remote(part, part, c_s, c_r, wide_2=other).start()
+
+        def forward(k, late=False):
+            for e in (2, side, 4 - side) if late else (side, 4 - side, 2):
+                x_copy(buf, x_s, x_r, e, k).start()
+            across(0, k)
 
         def landed(d):
-            b = block_of(d)
-            remote(buf.at[b, c], buf.at[b, c], z_s.at[d], z_r.at[d], wide_1=z).wait_recv()
-
-        def across(b):
-            remote(buf.at[b, c], buf.at[b, c], c_s, c_r, wide_2=other).start()
-
-        def arrived(d, onward=()):
+            z_copy(buf, z_s, z_r, d, 0).wait_recv()
+
+        def arrived(k):
             for e in (1, 3, 2):
-                b = lax.rem(x + NX - e, NX) * NZ + lax.rem(z + NZ - d, NZ)
-                remote(
-                    buf.at[b, c], buf.at[b, c], x_s.at[e, d], x_r.at[e, d], wide_0=x
-                ).wait_recv()
-                for n in onward:
-                    to = lax.rem(z + NZ + n - d, NZ)
-                    remote(buf.at[b, c], buf.at[b, c], x_s.at[e, n], x_r.at[e, n], wide_1=to).start()
-                across(b)
+                x_copy(buf, x_s, x_r, e, k).wait_recv()
+                across(e, k)
 
         for d in range(NEAR, 0, -1):
-            z_copy(buf, z_s, z_r, d).start()
-            z_copy(buf, z_s, z_r, NZ - d).start()
+            z_copy(buf, z_s, z_r, 0, d).start()
+            z_copy(buf, z_s, z_r, 0, NZ - d).start()
         forward(0)
-        across(chip)
-        for d in range(1, NEAR + 1):
-            for o in (d, NZ - d):
-                landed(o)
-                if d == NEAR:
-                    for n in range(NEAR, 0, -1):
-                        if o == NEAR:
-                            z_relay(buf, z_s, z_r, o, NEAR + n).start()
-                        elif NEAR + n < NZ // 2:
-                            z_relay(buf, z_s, z_r, o, NZ - NEAR - n).start()
-                forward(o)
-                across(block_of(o))
-        arrived(0)
-        arrived(4, (6, 5))
-        arrived(12, (10, 11))
-        for o in (7, 9, 8):
-            landed(o)
-            forward(o, (2, 1, 3))
-            across(block_of(o))
-        for o in (5, 11, 6, 10):
-            landed(o)
-            across(block_of(o))
+        landed(NEAR)
+        for hop in RELAY_HOPS:
+            z_copy(buf, z_s, z_r, NEAR, hop).start()
+        landed(NZ - NEAR)
+        for hop in RELAY_HOPS:
+            if NEAR + hop < NZ // 2:
+                z_copy(buf, z_s, z_r, NZ - NEAR, NZ - hop).start()
+        for k, (a, n) in enumerate(RUNS):
+            if k == 0:
+                continue
+            if k == 1 + len(NEAR_RUNS):
+                arrived(0)
+            for d in range(a, a + n):
+                if d not in (NEAR, NZ - NEAR):
+                    landed(d)
+            forward(k, k > len(NEAR_RUNS))
         if meanwhile is not None:
             meanwhile()
-
-        def arrived_pair(d):
-            arrived(d)
-            arrived(NZ - d)
-
-        loop(NEAR, arrived_pair, 1)
-        loop(NZ // 2, arrived_pair, NEAR + 1)
-        arrived(NZ // 2)
-        remote(buf.at[:, other], buf.at[:, other], c_s, c_r, wide_2=other).wait_recv()
+        for k in range(1, len(RUNS)):
+            arrived(k)
+        part = buf.at[:, other]
+        remote(part, part, c_s, c_r, wide_2=other).wait_recv()
 
     def gather_sent(buf, z_s, z_r, x_s, x_r, c_s, c_r):
-        def far(d):
-            z_copy(buf, z_s, z_r, d).wait_send()
-
-        loop(NZ, far, 1)
-
-        def near(d):
+        for d in range(1, NZ):
+            z_copy(buf, z_s, z_r, 0, d).wait_send()
+        for k in range(len(RUNS)):
             for e in range(1, NX):
-                x_copy(buf, x_s, x_r, e, d).wait_send()
-
-        loop(NZ, near)
-        remote(buf.at[:, c], buf.at[:, c], c_s, c_r, wide_2=other).wait_send()
+                x_copy(buf, x_s, x_r, e, k).wait_send()
+        part = buf.at[:, c]
+        remote(part, part, c_s, c_r, wide_2=other).wait_send()
+
+    def tall(buf, i, h, t):
+        e = lax.rem(x + NX - i, NX)
+        return jnp.concatenate(
+            [buf[e, h, lax.rem(z + NZ - b, NZ), t].astype(F32) for b in range(NZ)], axis=0
+        )
 
     swap.wait_recv()
     mine, theirs = ex[...], exr[...]
@@ -240,7 +223,7 @@
         [jnp.where(first, mine, theirs), jnp.where(first, theirs, mine)], axis=1
     )
     half = jnp.where(first, rows8[:, :, :HALF], rows8[:, :, HALF:])
-    wbuf[chip, c] = half[:3].astype(BF16)
+    wbuf[0, c, 0] = half[:3].astype(BF16)
     mhalf[...] = half[3:]
 
     def turn_keys():
@@ -251,11 +234,9 @@
 
     def square(i):
         r = pl.ds(pl.multiple_of(i * TOK, TOK), TOK)
-        b = pl.ds(pl.multiple_of(i * NZ, NZ), NZ)
         for t in range(3):
             for h in range(2):
-                part = wbuf[b, h, t].astype(F32).reshape(TOK, HALF)
-                w2[t, r, h * HALF : (h + 1) * HALF] = part.astype(BF16)
+                w2[t, r, h * HALF : (h + 1) * HALF] = tall(wbuf, i, h, t).astype(BF16)
 
     loop(4, square)
     tok_wait(1)
@@ -306,7 +287,7 @@
         for b in range(NX):
             for t in range(3):
                 xs[b, p, t] = (own[p, b, t] + grecv[p, b, t].astype(F32)).astype(BF16)
-        for e in (1, 3, 2):
+        for e in (side, 4 - side, 2):
             rx_copy(j, e).start()
 
     def grad_and_pair(j):
@@ -368,13 +349,12 @@
         return total + zr[frm].astype(F32)
 
     total = lax.fori_loop(1, NZ, summed, zr[z].astype(F32))
-    mbuf[chip, c] = (momentum_decay * mhalf[...] + total * TOKENS**-0.5).astype(BF16)
+    mbuf[0, c, 0] = (momentum_decay * mhalf[...] + total * TOKENS**-0.5).astype(BF16)
     gather(mbuf, mz_s, mz_r, mx_s, mx_r, mc_s, mc_r)
 
     def squares(i, sums):
-        b = pl.ds(pl.multiple_of(i * NZ, NZ), NZ)
         return tuple(
-            s + jnp.sum(jnp.square(mbuf[b, 0, t].astype(F32)) + jnp.square(mbuf[b, 1, t].astype(F32)), axis=0)
+            s + jnp.sum(jnp.square(mbuf[i, 0, :, t].astype(F32)) + jnp.square(mbuf[i, 1, :, t].astype(F32)), axis=0)
             for t, s in enumerate(sums)
         )
 
@@ -395,16 +375,8 @@
 
     def renew(i):
         r = pl.ds(pl.multiple_of(i * TOK, TOK), TOK)
-        b = pl.ds(pl.multiple_of(i * NZ, NZ), NZ)
         for t in range(3):
-            parts = moved_rows(
-                *(
-                    buf[b, h, t].astype(F32).reshape(TOK, HALF)
-                    for buf in (wbuf, mbuf)
-                    for h in range(2)
-                ),
-                steps[t],
-            )
+            parts = moved_rows(*(tall(buf, i, h, t) for buf in (wbuf, mbuf) for h in range(2)), steps[t])
             for h in range(2):
                 n2[t, r, h * HALF : (h + 1) * HALF] = parts[h].astype(BF16)
 
@@ -413,7 +385,8 @@
         tok_copy(2, d).wait_send()
 
     def turn(i):
-        return 1 + 2 * i - 3 * lax.div(i, 2)
+        late = lax.div(i, 2)
+        return (1 - late) * lax.rem(1 + 2 * i + 2 * c, 4) + late * (2 * i - 2)
 
     def o_copy(i):
         to = lax.rem(y + turn(i), NY)
@@ -437,8 +410,8 @@
     keep.start()
 
     for t in range(3):
-        m0, m1 = mbuf[chip, 0, t].astype(F32), mbuf[chip, 1, t].astype(F32)
-        parts = moved_rows(wbuf[chip, 0, t].astype(F32), wbuf[chip, 1, t].astype(F32), m0, m1, steps[t])
+        m0, m1 = mbuf[0, 0, 0, t].astype(F32), mbuf[0, 1, 0, t].astype(F32)
+        parts = moved_rows(wbuf[0, 0, 0, t].astype(F32), wbuf[0, 1, 0, t].astype(F32), m0, m1, steps[t])
         whole = jnp.concatenate(parts, axis=1)
         newv[t] = jnp.where(first, whole[:4], whole[4:]).astype(BF16)
         whole = jnp.concatenate([m0, m1], axis=1)
@@ -465,8 +438,8 @@
 
     loop(NZ, z_sent, 1)
     gather_sent(mbuf, mz_s, mz_r, mx_s, mx_r, mc_s, mc_r)
-    for i, d in enumerate((1, 3, 2)):
-        frm = lax.rem(y + NY - d, NY)
+    for i in range(NY - 1):
+        frm = lax.rem(y + NY - turn(i), NY)
         remote(oblk.at[i], out.at[:, cols(frm)], o_s.at[i], o_r.at[i], narrow=frm).wait()
     keep.wait()
     for copy in done:
@@ -499,7 +472,7 @@
     dma = pltpu.SemaphoreType.DMA
     sq = (HEAD, HEAD)
     row = (4, HEAD)
-    gather_sems = [dma((NZ,)), dma((NZ,)), dma((NX, NZ)), dma((NX, NZ)), dma, dma]
+    gather_sems = [dma((NZ,)), dma((NZ,)), dma((NX, len(RUNS))), dma((NX, len(RUNS))), dma, dma]
     parts = pl.pallas_call(
         kernel,
         out_shape=(
@@ -520,7 +493,7 @@
             pltpu.VMEM((6, *row), F32),
             pltpu.VMEM((6, *row), F32),
             pltpu.VMEM((3, 8, HALF), F32),
-            pltpu.VMEM((CHIPS, 2, 3, 8, HALF), BF16),
+            pltpu.VMEM((NX, 2, NZ, 3, 8, HALF), BF16),
             pltpu.VMEM((3, HEAD, HEAD), BF16),
             pltpu.VMEM((4, NX, 3, 32, HALF), F32),
             pltpu.VMEM((4, NX, 3, 32, HALF), BF16),
@@ -529,7 +502,7 @@
             pltpu.VMEM((NX, 4, 3, 32, HALF), BF16),
             pltpu.VMEM((NZ, 3, 8, HALF), BF16),
             pltpu.VMEM((NZ, 3, 8, HALF), BF16),
-            pltpu.VMEM((CHIPS, 2, 3, 8, HALF), BF16),
+            pltpu.VMEM((NX, 2, NZ, 3, 8, HALF), BF16),
             pltpu.VMEM((3, HEAD, HEAD), BF16),
             pltpu.VMEM(sq, BF16),
             pltpu.VMEM((NY, TOK, HEAD), BF16),

time: 88.1 us -> 86.4 us (0.981)
  Pallas kernels: 87.2 us -> 85.5 us
    pallas_call x1, Pallas kernels: 85.3 us -> 83.5 us  [per_device(): pl.pallas_call(kernel, out_shape=(jax.ShapeDtypeStruct(queries.shape, BF1...]
where the time goes in v4:
time: 86.4 us; the launch traced here: 86.1 us
  Pallas kernels  85.5 us (99%)
    pallas_call x1, Pallas kernels, per_device(): pl.pallas_call(kernel, out_shape=(jax.ShapeDtypeStruct(queries.shape, BF1...  83.5 us
    pallas_call x1, Pallas kernels, per_device(): pl.pallas_call(deliver, out_shape=(jax.ShapeDtypeStruct(queries.shape, BF...  1.93 us

profile of v4, /device:TPU:1, one launch (start us, length us, event | category | flops | bytes accessed | tf_op | source)
XLA Modules:
  0.0 86.1 jit_solution(12552182092661514076)
XLA Ops:
  0.6 83.5 %shard_map.162 = (bf16[128,2048]{1,0:T(8,128)(2,1)}, bf16[3,4,512]{2,1,0:T(4,128)(2,1)}, f32[3,4,512]{2,1,0:T(4,128)}) custom-call(bf16[128,2048]{1,0:T(8,128)(2,1)} %q_in.1, bf16[128,2048]{1,0:T(8,128)(2,1)} %k_in.1, bf16[128,2048]{1,0:T(8,128)(2,1)} %v_in.1, s32[1,4]{1,0:T(1,128)} %lengths_in.1, f32[1,2048]{1,0:T(1,128)} %bitcast.1, ...), custom_call_target="tpu_custom_call" | custom-call | tf_op jit(solution)/shard_map/pallas_call | solution.py:476
  84.2 1.9 %shard_map.163 = (bf16[128,2048]{1,0:T(8,128)(2,1)}, bf16[1,4,512]{2,1,0:T(4,128)(2,1)}, bf16[1,4,512]{2,1,0:T(4,128)(2,1)}, bf16[1,4,512]{2,1,0:T(4,128)(2,1)},...) custom-call(bf16[128,2048]{1,0:T(8,128)(2,1)} %get-tuple-element.10.out_in, ...), custom_call_target="tpu_custom_call" | custom-call | tf_op jit(solution)/shard_map/pallas_call | solution.py:519

commit v5 on v4

--- a/solution.py
+++ b/solution.py
@@ -17,12 +17,14 @@
 epsilon = 1e-06
 
 NX, NZ, NY = 4, 16, 4
-NEAR = 4
-RELAY_HOPS = (1, 2, 3, 4)
-OWN_RUN = (0, 1)
-NEAR_RUNS = ((1, 4), (12, 4))
-FAR_RUNS = ((5, 2), (10, 2), (7, 3))
-RUNS = (OWN_RUN, *NEAR_RUNS, *FAR_RUNS)
+NEAR = 3
+STAGES = tuple(range(NEAR, NZ // 2, NEAR))
+LAST = STAGES[-1] + 1
+RUNS = (
+    (0, 1),
+    *((a, NEAR) for p in STAGES for a in (p - NEAR + 1, NZ - p)),
+    (LAST, NZ + 1 - 2 * LAST),
+)
 HEAD = 512
 HALF = 256
 GROUP = 512
@@ -174,26 +176,34 @@
                 x_copy(buf, x_s, x_r, e, k).wait_recv()
                 across(e, k)
 
-        for d in range(NEAR, 0, -1):
-            z_copy(buf, z_s, z_r, 0, d).start()
-            z_copy(buf, z_s, z_r, 0, NZ - d).start()
+        def onward(p):
+            hops = range(min(NEAR, NZ // 2 - p), 0, -1)
+            for hop in hops:
+                z_copy(buf, z_s, z_r, p, hop).start()
+
+        def backward(p):
+            for hop in range(min(NEAR, NZ // 2 - 1 - p), 0, -1):
+                z_copy(buf, z_s, z_r, (NZ - p) % NZ, NZ - hop).start()
+
+        onward(0)
+        backward(0)
         forward(0)
-        landed(NEAR)
-        for hop in RELAY_HOPS:
-            z_copy(buf, z_s, z_r, NEAR, hop).start()
-        landed(NZ - NEAR)
-        for hop in RELAY_HOPS:
-            if NEAR + hop < NZ // 2:
-                z_copy(buf, z_s, z_r, NZ - NEAR, NZ - hop).start()
-        for k, (a, n) in enumerate(RUNS):
+        for k, p in enumerate(STAGES):
+            landed(p)
+            onward(p)
+            landed(NZ - p)
+            backward(p)
+            for d in range(p - NEAR + 1, p):
+                landed(d)
+            forward(2 * k + 1)
+            for d in range(NZ - p + 1, NZ - p + NEAR):
+                landed(d)
+            forward(2 * k + 2)
             if k == 0:
-                continue
-            if k == 1 + len(NEAR_RUNS):
                 arrived(0)
-            for d in range(a, a + n):
-                if d not in (NEAR, NZ - NEAR):
-                    landed(d)
-            forward(k, k > len(NEAR_RUNS))
+        for d in range(LAST, NZ + 1 - LAST):
+            landed(d)
+        forward(len(RUNS) - 1, True)
         if meanwhile is not None:
             meanwhile()
         for k in range(1, len(RUNS)):

time: 86.4 us -> 85.7 us (level)
  no operation moved by 1% of the time
where the time goes in v5:
time: 85.7 us; the launch traced here: 85.5 us
  Pallas kernels  84.8 us (99%)
    pallas_call x1, Pallas kernels, per_device(): pl.pallas_call(kernel, out_shape=(jax.ShapeDtypeStruct(queries.shape, BF1...  82.9 us
    pallas_call x1, Pallas kernels, per_device(): pl.pallas_call(deliver, out_shape=(jax.ShapeDtypeStruct(queries.shape, BF...  1.93 us

profile of v5, /device:TPU:1, one launch (start us, length us, event | category | flops | bytes accessed | tf_op | source)
XLA Modules:
  0.0 85.5 jit_solution(2145046895784648291)
XLA Ops:
  0.6 82.9 %shard_map.162 = (bf16[128,2048]{1,0:T(8,128)(2,1)}, bf16[3,4,512]{2,1,0:T(4,128)(2,1)}, f32[3,4,512]{2,1,0:T(4,128)}) custom-call(bf16[128,2048]{1,0:T(8,128)(2,1)} %q_in.1, bf16[128,2048]{1,0:T(8,128)(2,1)} %k_in.1, bf16[128,2048]{1,0:T(8,128)(2,1)} %v_in.1, s32[1,4]{1,0:T(1,128)} %lengths_in.1, f32[1,2048]{1,0:T(1,128)} %bitcast.1, ...), custom_call_target="tpu_custom_call" | custom-call | tf_op jit(solution)/shard_map/pallas_call | solution.py:486
  83.5 1.9 %shard_map.163 = (bf16[128,2048]{1,0:T(8,128)(2,1)}, bf16[1,4,512]{2,1,0:T(4,128)(2,1)}, bf16[1,4,512]{2,1,0:T(4,128)(2,1)}, bf16[1,4,512]{2,1,0:T(4,128)(2,1)},...) custom-call(bf16[128,2048]{1,0:T(8,128)(2,1)} %get-tuple-element.10.out_in, ...), custom_call_target="tpu_custom_call" | custom-call | tf_op jit(solution)/shard_map/pallas_call | solution.py:529

commit v6 on v5

--- a/solution.py
+++ b/solution.py
@@ -351,7 +351,6 @@
 
     loop(4, fold)
     zr[z] = zs[z]
-    gather_sent(wbuf, wz_s, wz_r, wx_s, wx_r, wc_s, wc_r)
 
     def summed(d, total):
         frm = lax.rem(z + NZ - d, NZ)
@@ -391,8 +390,6 @@
                 n2[t, r, h * HALF : (h + 1) * HALF] = parts[h].astype(BF16)
 
     loop(4, renew)
-    for d in range(1, NY):
-        tok_copy(2, d).wait_send()
 
     def turn(i):
         late = lax.div(i, 2)
@@ -434,7 +431,7 @@
         copy.start()
 
     swap.wait_send()
-    for t in range(2):
+    for t in range(3):
         for d in range(1, NY):
             tok_copy(t, d).wait_send()
     for b in range(NX):
@@ -447,6 +444,7 @@
         rz_copy(lax.rem(z + d, NZ)).wait_send()
 
     loop(NZ, z_sent, 1)
+    gather_sent(wbuf, wz_s, wz_r, wx_s, wx_r, wc_s, wc_r)
     gather_sent(mbuf, mz_s, mz_r, mx_s, mx_r, mc_s, mc_r)
     for i in range(NY - 1):
         frm = lax.rem(y + NY - turn(i), NY)

time: 85.7 us -> 85.7 us (level)
  no operation moved by 1% of the time
where the time goes in v6:
time: 85.7 us; the launch traced here: 85.5 us
  Pallas kernels  84.8 us (99%)
    pallas_call x1, Pallas kernels, per_device(): pl.pallas_call(kernel, out_shape=(jax.ShapeDtypeStruct(queries.shape, BF1...  82.9 us
    pallas_call x1, Pallas kernels, per_device(): pl.pallas_call(deliver, out_shape=(jax.ShapeDtypeStruct(queries.shape, BF...  1.93 us

profile of v6, /device:TPU:1, one launch (start us, length us, event | category | flops | bytes accessed | tf_op | source)
XLA Modules:
  0.0 85.5 jit_solution(6914858260351475405)
XLA Ops:
  0.6 82.9 %shard_map.162 = (bf16[128,2048]{1,0:T(8,128)(2,1)}, bf16[3,4,512]{2,1,0:T(4,128)(2,1)}, f32[3,4,512]{2,1,0:T(4,128)}) custom-call(bf16[128,2048]{1,0:T(8,128)(2,1)} %q_in.1, bf16[128,2048]{1,0:T(8,128)(2,1)} %k_in.1, bf16[128,2048]{1,0:T(8,128)(2,1)} %v_in.1, s32[1,4]{1,0:T(1,128)} %lengths_in.1, f32[1,2048]{1,0:T(1,128)} %bitcast.1, ...), custom_call_target="tpu_custom_call" | custom-call | tf_op jit(solution)/shard_map/pallas_call | solution.py:484
  83.5 1.9 %shard_map.163 = (bf16[128,2048]{1,0:T(8,128)(2,1)}, bf16[1,4,512]{2,1,0:T(4,128)(2,1)}, bf16[1,4,512]{2,1,0:T(4,128)(2,1)}, bf16[1,4,512]{2,1,0:T(4,128)(2,1)},...) custom-call(bf16[128,2048]{1,0:T(8,128)(2,1)} %get-tuple-element.10.out_in, ...), custom_call_target="tpu_custom_call" | custom-call | tf_op jit(solution)/shard_map/pallas_call | solution.py:527
